TPU v7x, 128 devices: a whole 4x4x4 slice. The times are simulated.
128 devices in a mesh: dp: 8 (over y, core), pipe: 4 (over x), tensor: 4 (over z).
Axes of the slice: x: 4, y: 4, z: 4, core: 2. Of those that a mesh axis runs over, the one named last changes fastest.
Arguments:
- query_states: bfloat16 [16, 512, 1024], P('dp'), may hold values from -6 to 6
- doc_states: bfloat16 [16, 512, 1024], P('dp'), may hold values from -6 to 6
- query_len: int32 [16], P('dp'), may hold values from 64 to 512
- doc_len: int32 [16], P('dp'), may hold values from 64 to 512
- doc_order: int32 [8, 2], P('dp'), may hold values from 0 to 1, each once within a row
- w_qkv: bfloat16 [4, 3, 1024, 1024], P('pipe', None, None, 'tensor'), may hold values from -0.1875 to 0.1875
- w_out: bfloat16 [4, 1024, 1024], P('pipe', 'tensor'), may hold values from -0.1875 to 0.1875
- w_up: bfloat16 [4, 1024, 4096], P('pipe', None, 'tensor'), may hold values from -0.1875 to 0.1875
- w_down: bfloat16 [4, 4096, 1024], P('pipe', 'tensor'), may hold values from -0.09375 to 0.09375
- gain_attn: float32 [4, 1024], P('pipe'), may hold values from 0.1 to 1.9
- gain_mlp: float32 [4, 1024], P('pipe'), may hold values from 0.1 to 1.9
Outputs:
- query_vectors: bfloat16 [16, 1024], P('dp', ('pipe', 'tensor'))
- document_vectors: bfloat16 [16, 1024], P('dp', ('pipe', 'tensor'))
- pair_loss: float32 [16], P('dp')
Inputs may be any that keep to these rules, and one draw needn't show every extreme that they name: `doc_order`: each row holds every number of 0 to 1 once.
All inputs are finite; a program needn't handle non-finite values.
Results may differ from a plain program's by a relative error of at most 0.035.
Values may be sent and summed in bfloat16 or wider, within the bound.
A program may use at most 192 MiB of HBM per device.

v0:
```python
import math

import jax
import jax.numpy as jnp
from jax import lax
from jax.sharding import PartitionSpec as P

D = 1024
HEADS = 16


SOFTMAX_TEMPER = 0.05
EPSILON = 1e-06
LAYER_EPSILON = 1e-12


def from_behind(value, axis, steps):
    count = lax.axis_size(axis)
    initial, last = (max(0, -steps), min(count, count - steps))
    return lax.ppermute(value, axis, [(source, source + steps) for source in range(initial, last)])


def from_root(x, axis, root):
    return lax.dynamic_index_in_dim(lax.all_gather(x, axis), root, 0, keepdims=False)


def laid_out(parts, dim):
    lengths = list(parts.shape[1:])
    lengths[dim] *= parts.shape[0]
    return jnp.moveaxis(parts, 0, dim).reshape(lengths)


def copy_for_each(x, axis):
    peers = lax.axis_size(axis)
    return lax.all_to_all(jnp.broadcast_to(x[None], (peers, *x.shape)), axis, 0, 0, tiled=True)


def collect(x, axis, dim):
    return laid_out(copy_for_each(x, axis), dim)


def of_everyone(x, axis):
    return copy_for_each(x, axis).sum(axis=0)


def norm_rows(values_in, gain_row):
    row_mean = jnp.mean(values_in, axis=-1, keepdims=True)
    centered = values_in - row_mean
    variance = jnp.mean(centered * centered, axis=-1, keepdims=True)
    return centered * lax.rsqrt(variance + LAYER_EPSILON) * gain_row


def local_reduce(left_side, right_side, residual, gain_row, group_count):
    row_total = left_side.shape[0]
    group_width = left_side.shape[1] // group_count
    left_parts = left_side.reshape(row_total, group_count, group_width)
    right_parts = right_side.reshape(group_count, group_width, right_side.shape[1])
    partials = jnp.einsum(
        "sgk,gkd->gsd", left_parts, right_parts, preferred_element_type=jnp.float32
    )
    summed = jnp.sum(partials.astype(jnp.bfloat16).astype(jnp.float32), axis=0)
    return norm_rows(residual.astype(jnp.float32) + summed, gain_row).astype(jnp.bfloat16)


def reduce_block(left_side, right_side, residual, gain_row, group_count):
    return local_reduce(left_side, right_side, residual, gain_row, group_count)


def encode_layer(hidden, valid_keys, w_qkv, w_out, w_up, w_down, gain_attn, gain_mlp, group_count):
    head_width = D // HEADS
    local_width = w_qkv.shape[-1]
    head_count = local_width // head_width
    slot_count = hidden.shape[0]
    inv_sqrt = 1.0 / math.sqrt(head_width)
    query_rows = (jnp.dot(hidden, w_qkv[0], preferred_element_type=jnp.float32) * inv_sqrt).astype(
        jnp.bfloat16
    )
    key_rows = jnp.dot(hidden, w_qkv[1], preferred_element_type=jnp.float32).astype(jnp.bfloat16)
    value_rows = jnp.dot(hidden, w_qkv[2], preferred_element_type=jnp.float32).astype(jnp.bfloat16)
    query_heads = query_rows.reshape(slot_count, head_count, head_width)
    key_heads = key_rows.reshape(slot_count, head_count, head_width)
    value_heads = value_rows.reshape(slot_count, head_count, head_width)
    scores = jnp.einsum("qhe,khe->hqk", query_heads, key_heads, preferred_element_type=jnp.float32)
    exp_scores = jnp.where(valid_keys[None, None, :], jnp.exp(scores), 0.0)
    attention = (exp_scores / jnp.sum(exp_scores, axis=-1, keepdims=True)).astype(jnp.bfloat16)
    context = jnp.einsum("hqk,khe->qhe", attention, value_heads, preferred_element_type=jnp.float32)
    context = context.astype(jnp.bfloat16).reshape(slot_count, local_width)
    mixed = reduce_block(context, w_out, hidden, gain_attn, group_count)
    upward = jnp.dot(mixed, w_up, preferred_element_type=jnp.float32)
    activated = jax.nn.gelu(upward, approximate=False).astype(jnp.bfloat16)
    return reduce_block(activated, w_down, mixed, gain_mlp, group_count)


def interior_rows(left_side, right_side):
    return lax.dot_general(
        left_side, right_side, (((1,), (1,)), ((), ())), preferred_element_type=jnp.float32
    )


def per_device(
    query_states,
    doc_states,
    query_len,
    doc_len,
    doc_order,
    w_qkv,
    w_out,
    w_up,
    w_down,
    gain_attn,
    gain_mlp,
):
    pair_count = query_states.shape[0]
    seq_count = 2 * pair_count
    slot_count = query_states.shape[1]
    model_width = query_states.shape[2]
    section_count = lax.axis_size("pipe")
    section_index = lax.axis_index("pipe")
    tensor_count = lax.axis_size("tensor")
    lengths = jnp.concatenate([query_len, doc_len])
    positions = jnp.arange(slot_count, dtype=jnp.int32)
    piece_width = model_width // (section_count * tensor_count)
    w_qkv, w_out, w_up, w_down = (
        lax.all_gather(w_qkv, "tensor", axis=3, tiled=True),
        lax.all_gather(w_out, "tensor", axis=1, tiled=True),
        lax.all_gather(w_up, "tensor", axis=2, tiled=True),
        lax.all_gather(w_down, "tensor", axis=1, tiled=True),
    )
    share = seq_count // tensor_count
    first_seq = lax.axis_index("tensor") * share
    local_ids = jnp.arange(share, dtype=jnp.int32)

    def tick_step(tick_index, state_pair):
        passed, pooled = state_pair
        entry_index = first_seq + jnp.clip(tick_index, 0, share - 1)
        query_pick = query_states[jnp.minimum(entry_index, pair_count - 1)]
        doc_pick = doc_states[jnp.clip(entry_index - pair_count, 0, pair_count - 1)]
        fresh = jnp.where(entry_index < pair_count, query_pick, doc_pick)
        hidden = jnp.where(section_index == 0, fresh, passed)
        local_index = jnp.clip(tick_index - section_index, 0, share - 1)
        seq_length = lengths[first_seq + local_index]
        valid_keys = positions < seq_length
        hidden = encode_layer(
            hidden,
            valid_keys,
            w_qkv[0],
            w_out[0],
            w_up[0],
            w_down[0],
            gain_attn[0],
            gain_mlp[0],
            tensor_count,
        )
        finished = tick_index - (section_count - 1)
        store_now = (section_index == section_count - 1) & (finished >= 0)
        summed = jnp.sum(jnp.where(valid_keys[:, None], hidden.astype(jnp.float32), 0.0), axis=0)
        mean_row = summed / seq_length.astype(jnp.float32)
        row_mask = (local_ids == local_index) & store_now
        pooled = jnp.where(row_mask[:, None], mean_row[None, :], pooled)
        passed = from_behind(hidden, "pipe", 1)
        return (passed, pooled)

    start_pair = (
        jnp.zeros((slot_count, model_width), jnp.bfloat16),
        jnp.zeros((share, model_width), jnp.float32),
    )
    unused_state, pooled = lax.fori_loop(0, share + section_count - 1, tick_step, start_pair)
    embedded = (
        pooled * lax.rsqrt(jnp.sum(pooled * pooled, axis=1, keepdims=True) + EPSILON)
    ).astype(jnp.bfloat16)
    grouped = embedded.reshape(share, section_count, tensor_count, piece_width)
    moved = lax.all_to_all(grouped, "tensor", split_axis=2, concat_axis=0, tiled=True)
    tensor_cols = moved.reshape(seq_count, section_count, piece_width)
    shared = from_root(tensor_cols, "pipe", section_count - 1)
    own_piece = lax.dynamic_index_in_dim(shared, section_index, 1, keepdims=False)
    query_portion = own_piece[:pair_count]
    document_portion = own_piece[pair_count:]
    order_row = doc_order[0]
    data_count = lax.axis_size("dp")
    partial_table = interior_rows(query_portion, collect(document_portion, "dp", 0))
    score_table = of_everyone(partial_table, ("pipe", "tensor")) / SOFTMAX_TEMPER
    column_ids = jnp.arange(pair_count * data_count, dtype=jnp.int32)
    target = lax.axis_index("dp") * pair_count + order_row
    is_positive = column_ids[None, :] == target[:, None]
    positive_score = jnp.sum(jnp.where(is_positive, score_table, 0.0), axis=1)
    exp_total = jnp.sum(jnp.exp(score_table), axis=1)
    pair_loss = jnp.log(exp_total) - positive_score
    return (query_portion, document_portion, pair_loss)


def solution(mesh):
    in_specs = (
        P("dp", None, None),
        P("dp", None, None),
        P("dp"),
        P("dp"),
        P("dp", None),
        P("pipe", None, None, "tensor"),
        P("pipe", "tensor", None),
        P("pipe", None, "tensor"),
        P("pipe", "tensor", None),
        P("pipe", None),
        P("pipe", None),
    )
    out_specs = (P("dp", ("pipe", "tensor")), P("dp", ("pipe", "tensor")), P("dp"))
    return jax.shard_map(
        per_device, mesh=mesh, in_specs=in_specs, out_specs=out_specs, check_vma=False
    )
```

profile of v0, /device:TPU:0, one launch (start us, length us, event | category | flops | bytes accessed | tf_op | source)
XLA Modules:
  0.0 658.8 jit_solution(12119853464796553148)
XLA Ops:
  10.7 32.4 %all-gather.8.cloned.1.call-done = bf16[1,1024,1024]{2,1,0:T(8,128)(2,1)} async-done(((bf16[1,256,1024]{2,1,0:T(8,128)(2,1)}), bf16[1,1024,1024]{2,1,0:T(8,128)(2,1)}) %all-gather.8.cloned.1.call-update) | async-done | bytes 2097168 | tf_op jit(solution)/shard_map/all_gather | solution.py:125
  43.2 70.9 %all-gather.6.cloned.1.call-done = bf16[1,3,1024,1024]{3,2,1,0:T(8,128)(2,1)} async-done(((bf16[1,3,1024,256]{3,2,1,0:T(8,128)(2,1)}), bf16[1,3,1024,1024]{3,2,1,0:T(8,128)(2,1)}) %all-gather.6.cloned.1.call-update) | async-done | bytes 6291472 | tf_op jit(solution)/shard_map/all_gather | solution.py:124
  114.0 85.5 %all-gather.10.cloned.1.call-done = bf16[1,1024,4096]{2,1,0:T(8,128)(2,1)} async-done(((bf16[1,1024,1024]{2,1,0:T(8,128)(2,1)}), bf16[1,1024,4096]{2,1,0:T(8,128)(2,1)}) %all-gather.10.cloned.1.call-update) | async-done | bytes 8388624 | tf_op jit(solution)/shard_map/all_gather | solution.py:126
  199.5 85.6 %all-gather.12.cloned.1.call-done = bf16[1,4096,1024]{2,1,0:T(8,128)(2,1)} async-done(((bf16[1,1024,1024]{2,1,0:T(8,128)(2,1)}), bf16[1,4096,1024]{2,1,0:T(8,128)(2,1)}) %all-gather.12.cloned.1.call-update) | async-done | bytes 8388624 | tf_op jit(solution)/shard_map/all_gather | solution.py:127
  285.3 318.5 %while.18 = (s32[]{:T(128)}, bf16[512,1024]{1,0:T(8,128)(2,1)S(1)}, f32[1,1024]{1,0:T(1,128)S(1)}, pred[]{:T(512)}, s32[]{:T(128)}, /*index=5*/bf16[2,512,1024]{...) while((s32[]{:T(128)}, bf16[512,1024]{1,0:T(8,128)(2,1)S(1)}, ...), condition=%wide.region_9.10_spmd.clone, body=%wide.region_0.9_spmd.clone.sunk | while | flops 14147382272 | bytes 201497376 | solution.py:167
  311.0 22.6 %fusion.96 = bf16[512,4096]{1,0:T(8,128)(2,1)S(1)} fusion(bf16[512,1024]{1,0:T(8,128)(2,1)S(1)} %multiply_convert_fusion.7, bf16[1,1024,4096]{2,1,0:T(8,128)(2,1)S(1)} %bitcast.137), kind=kOutput, calls=%fused_computation.7.clone.1 | convolution fusion | flops 4431282176 | bytes 13631488 | tf_op jit(solution)/shard_map/while/body/eval_jaxpr/dot_general | solution.py:89
  333.7 4.9 convert_reduce_fusion.6
  344.0 21.5 %collective-permute-done = bf16[512,1024]{1,0:T(8,128)(2,1)S(1)} collective-permute-done((bf16[512,1024]{1,0:T(8,128)(2,1)S(1)}, bf16[512,1024]{1,0:T(8,128)(2,1)S(1)}, u32[]{:S(2)}, u32[]{:S(2)}) %collective-permute-start) | collective-permute-done | bytes 1048608 | tf_op jit(solution)/shard_map/while/body/eval_jaxpr/ppermute | solution.py:20
  391.2 22.6 %fusion.96 = bf16[512,4096]{1,0:T(8,128)(2,1)S(1)} fusion(bf16[512,1024]{1,0:T(8,128)(2,1)S(1)} %multiply_convert_fusion.7, bf16[1,1024,4096]{2,1,0:T(8,128)(2,1)S(1)} %bitcast.137), kind=kOutput, calls=%fused_computation.7.clone.1 | convolution fusion | flops 4431282176 | bytes 13631488 | tf_op jit(solution)/shard_map/while/body/eval_jaxpr/dot_general | solution.py:89
  413.8 4.9 convert_reduce_fusion.6
  420.0 4.4 collective-permute-start
  425.2 20.6 %collective-permute-done = bf16[512,1024]{1,0:T(8,128)(2,1)S(1)} collective-permute-done((bf16[512,1024]{1,0:T(8,128)(2,1)S(1)}, bf16[512,1024]{1,0:T(8,128)(2,1)S(1)}, u32[]{:S(2)}, u32[]{:S(2)}) %collective-permute-start) | collective-permute-done | bytes 1048608 | tf_op jit(solution)/shard_map/while/body/eval_jaxpr/ppermute | solution.py:20
  471.5 22.6 %fusion.96 = bf16[512,4096]{1,0:T(8,128)(2,1)S(1)} fusion(bf16[512,1024]{1,0:T(8,128)(2,1)S(1)} %multiply_convert_fusion.7, bf16[1,1024,4096]{2,1,0:T(8,128)(2,1)S(1)} %bitcast.137), kind=kOutput, calls=%fused_computation.7.clone.1 | convolution fusion | flops 4431282176 | bytes 13631488 | tf_op jit(solution)/shard_map/while/body/eval_jaxpr/dot_general | solution.py:89
  494.1 4.9 convert_reduce_fusion.6
  500.3 4.4 collective-permute-start
  505.4 19.8 %collective-permute-done = bf16[512,1024]{1,0:T(8,128)(2,1)S(1)} collective-permute-done((bf16[512,1024]{1,0:T(8,128)(2,1)S(1)}, bf16[512,1024]{1,0:T(8,128)(2,1)S(1)}, u32[]{:S(2)}, u32[]{:S(2)}) %collective-permute-start) | collective-permute-done | bytes 1048608 | tf_op jit(solution)/shard_map/while/body/eval_jaxpr/ppermute | solution.py:20
  550.9 22.6 %fusion.96 = bf16[512,4096]{1,0:T(8,128)(2,1)S(1)} fusion(bf16[512,1024]{1,0:T(8,128)(2,1)S(1)} %multiply_convert_fusion.7, bf16[1,1024,4096]{2,1,0:T(8,128)(2,1)S(1)} %bitcast.137), kind=kOutput, calls=%fused_computation.7.clone.1 | convolution fusion | flops 4431282176 | bytes 13631488 | tf_op jit(solution)/shard_map/while/body/eval_jaxpr/dot_general | solution.py:89
  573.5 4.9 convert_reduce_fusion.6
  579.8 4.4 collective-permute-start
  584.9 18.9 %collective-permute-done = bf16[512,1024]{1,0:T(8,128)(2,1)S(1)} collective-permute-done((bf16[512,1024]{1,0:T(8,128)(2,1)S(1)}, bf16[512,1024]{1,0:T(8,128)(2,1)S(1)}, u32[]{:S(2)}, u32[]{:S(2)}) %collective-permute-start) | collective-permute-done | bytes 1048608 | tf_op jit(solution)/shard_map/while/body/eval_jaxpr/ppermute | solution.py:20
  609.9 5.3 all-to-all-done
  615.2 13.3 %all-gather = bf16[16,1,4,1,64]{4,2,3,1,0:T(4,128)(2,1)S(1)} all-gather(bf16[4,1,4,1,64]{4,2,3,1,0:T(4,128)(2,1)S(1)} %bitcast_bitcast_fusion), channel_id=2, replica_groups=mesh['dp'=8,'pipe'=4,'tensor'=4] {'pipe'}, dimensions={0}, use_global_device_ids=true | all-gather | bytes 10240 | tf_op jit(solution)/shard_map/all_gather | solution.py:24
  633.5 5.3 all-to-all-done.1
  643.9 7.6 %all-to-all-done.2 = f32[16,2,16]{2,1,0:T(2,128)S(1)} async-done(((f32[16,2,16]{2,1,0:T(2,128)}), f32[16,2,16]{2,1,0:T(2,128)S(1)}, u32[]{:S(2)}, u32[]{:S(2)}) %all-to-all-start.2) | async-done | bytes 2080 | tf_op jit(solution)/shard_map/all_to_all | solution.py:35
  (227 shorter events, 130.7 us)
Async XLA Ops:
  7.2 36.0 %all-gather.8.cloned.1.call-start = ((), (), s32[]{:S(2)}) async-start(), calls=%async_computation.4 | async-start | bytes 2621440 | tf_op jit(solution)/shard_map/all_gather | solution.py:125
  7.9 106.1 %all-gather.6.cloned.1.call-start = ((), (), s32[]{:S(2)}) async-start(), calls=%async_computation.3 | async-start | bytes 7864320 | tf_op jit(solution)/shard_map/all_gather | solution.py:124
  8.6 190.9 %all-gather.10.cloned.1.call-start = ((), (), s32[]{:S(2)}) async-start(), calls=%async_computation.5 | async-start | bytes 10485760 | tf_op jit(solution)/shard_map/all_gather | solution.py:126
  9.4 275.8 %all-gather.12.cloned.1.call-start = ((), (), s32[]{:S(2)}) async-start(), calls=%async_computation.6 | async-start | bytes 10485760 | tf_op jit(solution)/shard_map/all_gather | solution.py:127
  285.3 358.6 %copy-start.6 = (s32[1,2]{1,0:T(1,128)S(1)}, s32[1,2]{1,0:T(1,128)}, u32[]{:S(2)}) copy-start(s32[1,2]{1,0:T(1,128)} %param.17) | copy-start | bytes 28
  309.0 24.7 %slice-start.2 = ((s8[8388608]{0:T(1024)(128)(4,1)}), s8[4194304]{0:T(1024)(128)(4,1)S(1)}, s32[]{:S(2)}) async-start(s8[8388608]{0:T(1024)(128)(4,1)} %bitcast.138), calls=%async_computation.9 | async-start | bytes 8388608 | tf_op jit(solution)/shard_map/while
  311.0 22.6 %slice-start.3 = ((s8[8388608]{0:T(1024)(128)(4,1)}), s8[4194304]{0:T(1024)(128)(4,1)S(1)}, s32[]{:S(2)}) async-start(s8[8388608]{0:T(1024)(128)(4,1)} %bitcast.138), calls=%async_computation.10 | async-start | bytes 8388608 | tf_op jit(solution)/shard_map/while
  333.6 5.7 copy-start.1
  339.9 25.6 %collective-permute-start = (bf16[512,1024]{1,0:T(8,128)(2,1)S(1)}, bf16[512,1024]{1,0:T(8,128)(2,1)S(1)}, u32[]{:S(2)}, u32[]{:S(2)}) collective-permute-start(bf16[512,1024]{1,0:T(8,128)(2,1)S(1)} %get-tuple-element.564), channel_id=1, source_target_pairs={{0,4},{4,8},{8,12},{1,5},{5,9},{9,13},{2,6},{6,10},{10,14},{3,7},{... | collective-permute-start | bytes 3145736 | tf_op jit(solution)/shard_map/while/body/eval_jaxpr/ppermute | solution.py:20
  389.1 24.7 %slice-start.2 = ((s8[8388608]{0:T(1024)(128)(4,1)}), s8[4194304]{0:T(1024)(128)(4,1)S(1)}, s32[]{:S(2)}) async-start(s8[8388608]{0:T(1024)(128)(4,1)} %bitcast.138), calls=%async_computation.9 | async-start | bytes 8388608 | tf_op jit(solution)/shard_map/while
  391.2 22.6 %slice-start.3 = ((s8[8388608]{0:T(1024)(128)(4,1)}), s8[4194304]{0:T(1024)(128)(4,1)S(1)}, s32[]{:S(2)}) async-start(s8[8388608]{0:T(1024)(128)(4,1)} %bitcast.138), calls=%async_computation.10 | async-start | bytes 8388608 | tf_op jit(solution)/shard_map/while
  413.8 5.7 copy-start.1
  420.0 25.8 %collective-permute-start = (bf16[512,1024]{1,0:T(8,128)(2,1)S(1)}, bf16[512,1024]{1,0:T(8,128)(2,1)S(1)}, u32[]{:S(2)}, u32[]{:S(2)}) collective-permute-start(bf16[512,1024]{1,0:T(8,128)(2,1)S(1)} %get-tuple-element.564), channel_id=1, source_target_pairs={{0,4},{4,8},{8,12},{1,5},{5,9},{9,13},{2,6},{6,10},{10,14},{3,7},{... | collective-permute-start | bytes 3145736 | tf_op jit(solution)/shard_map/while/body/eval_jaxpr/ppermute | solution.py:20
  469.4 24.7 %slice-start.2 = ((s8[8388608]{0:T(1024)(128)(4,1)}), s8[4194304]{0:T(1024)(128)(4,1)S(1)}, s32[]{:S(2)}) async-start(s8[8388608]{0:T(1024)(128)(4,1)} %bitcast.138), calls=%async_computation.9 | async-start | bytes 8388608 | tf_op jit(solution)/shard_map/while
  471.5 22.6 %slice-start.3 = ((s8[8388608]{0:T(1024)(128)(4,1)}), s8[4194304]{0:T(1024)(128)(4,1)S(1)}, s32[]{:S(2)}) async-start(s8[8388608]{0:T(1024)(128)(4,1)} %bitcast.138), calls=%async_computation.10 | async-start | bytes 8388608 | tf_op jit(solution)/shard_map/while
  500.3 24.9 %collective-permute-start = (bf16[512,1024]{1,0:T(8,128)(2,1)S(1)}, bf16[512,1024]{1,0:T(8,128)(2,1)S(1)}, u32[]{:S(2)}, u32[]{:S(2)}) collective-permute-start(bf16[512,1024]{1,0:T(8,128)(2,1)S(1)} %get-tuple-element.564), channel_id=1, source_target_pairs={{0,4},{4,8},{8,12},{1,5},{5,9},{9,13},{2,6},{6,10},{10,14},{3,7},{... | collective-permute-start | bytes 3145736 | tf_op jit(solution)/shard_map/while/body/eval_jaxpr/ppermute | solution.py:20
  548.8 24.7 %slice-start.2 = ((s8[8388608]{0:T(1024)(128)(4,1)}), s8[4194304]{0:T(1024)(128)(4,1)S(1)}, s32[]{:S(2)}) async-start(s8[8388608]{0:T(1024)(128)(4,1)} %bitcast.138), calls=%async_computation.9 | async-start | bytes 8388608 | tf_op jit(solution)/shard_map/while
  550.9 22.6 %slice-start.3 = ((s8[8388608]{0:T(1024)(128)(4,1)}), s8[4194304]{0:T(1024)(128)(4,1)S(1)}, s32[]{:S(2)}) async-start(s8[8388608]{0:T(1024)(128)(4,1)} %bitcast.138), calls=%async_computation.10 | async-start | bytes 8388608 | tf_op jit(solution)/shard_map/while
  579.8 24.1 %collective-permute-start = (bf16[512,1024]{1,0:T(8,128)(2,1)S(1)}, bf16[512,1024]{1,0:T(8,128)(2,1)S(1)}, u32[]{:S(2)}, u32[]{:S(2)}) collective-permute-start(bf16[512,1024]{1,0:T(8,128)(2,1)S(1)} %get-tuple-element.564), channel_id=1, source_target_pairs={{0,4},{4,8},{8,12},{1,5},{5,9},{9,13},{2,6},{6,10},{10,14},{3,7},{... | collective-permute-start | bytes 3145736 | tf_op jit(solution)/shard_map/while/body/eval_jaxpr/ppermute | solution.py:20
  605.9 9.3 %all-to-all-start = ((bf16[4,2,128]{2,1,0:T(2,128)(2,1)}), bf16[4,2,128]{2,1,0:T(2,128)(2,1)S(1)}, u32[]{:S(2)}, u32[]{:S(2)}) async-start(bf16[4,2,128]{2,1,0:T(2,128)(2,1)} %reshape.179), calls=%async_computation | async-start | bytes 4096 | tf_op jit(solution)/shard_map/all_to_all | solution.py:172
  628.6 23.7 %copy-start.3 = (bf16[2,64]{1,0:T(2,128)(2,1)}, bf16[2,64]{1,0:T(2,128)(2,1)S(1)}, u32[]{:S(2)}) copy-start(bf16[2,64]{1,0:T(2,128)(2,1)S(1)} %get-tuple-element.459) | copy-start | bytes 772
  628.6 23.7 %copy-start.4 = (bf16[2,64]{1,0:T(2,128)(2,1)}, bf16[2,64]{1,0:T(2,128)(2,1)S(1)}, u32[]{:S(2)}) copy-start(bf16[2,64]{1,0:T(2,128)(2,1)S(1)} %get-tuple-element.460) | copy-start | bytes 772
  629.2 9.6 %all-to-all-start.1 = ((bf16[8,2,64]{2,1,0:T(2,128)(2,1)}), bf16[8,2,64]{2,1,0:T(2,128)(2,1)S(1)}, u32[]{:S(2)}, u32[]{:S(2)}) async-start(bf16[8,2,64]{2,1,0:T(2,128)(2,1)} %broadcast_in_dim.139), calls=%async_computation.1 | async-start | bytes 8192 | tf_op jit(solution)/shard_map/all_to_all | solution.py:35
  639.5 12.0 %all-to-all-start.2 = ((f32[16,2,16]{2,1,0:T(2,128)}), f32[16,2,16]{2,1,0:T(2,128)S(1)}, u32[]{:S(2)}, u32[]{:S(2)}) async-start(f32[16,2,16]{2,1,0:T(2,128)} %broadcast_in_dim.140), calls=%async_computation.2 | async-start | bytes 32768 | tf_op jit(solution)/shard_map/all_to_all | solution.py:35
  (30 other events, 99.3 us)
Sparse Core Ops, SparseCore 0:
  9.6 33.4 all-gather.7
  44.8 69.1 all-gather.5
  115.7 83.7 all-gather.9
  201.0 84.0 all-gather.11
where the time goes:
time: 659 us
  waiting for transfers between devices  376 us (57%)
  matrix products  173 us (26%)
  starting transfers between devices  29.6 us (4%)
  local copies, waits for them, and re-layouts  26.4 us (4%)
  other arithmetic  22.3 us (3%)
  between operations  14.6 us (2%)
  blocking collectives  13.3 us (2%)
    dot_general x4, matrix products, encode_layer(): upward = jnp.dot(mixed, w_up, preferred_element_type=jnp.float32)  90.3 us
    all_gather x1, waiting for transfers between devices, per_device(): lax.all_gather(w_down, 'tensor', axis=1, tiled=True)  85.6 us
    all_gather x1, waiting for transfers between devices, per_device(): lax.all_gather(w_up, 'tensor', axis=2, tiled=True)  85.5 us
    ppermute x4, waiting for transfers between devices, from_behind(): lax.ppermute(value, axis, [(source, source + steps) for source in range(i...  80.8 us
    all_gather x1, waiting for transfers between devices, per_device(): lax.all_gather(w_qkv, 'tensor', axis=3, tiled=True)  70.9 us
    all_gather x1, waiting for transfers between devices, per_device(): lax.all_gather(w_out, 'tensor', axis=1, tiled=True)  32.4 us
    dot_general x8, matrix products, local_reduce(): jnp.einsum('sgk,gkd->gsd', left_parts, right_parts, preferred_element_typ...  24.7 us
    ppermute x4, starting transfers between devices, from_behind(): lax.ppermute(value, axis, [(source, source + steps) for source in range(i...  16.8 us
  transfers between devices with their start and end apart: 11, of which 11 were waited for; matrix products, arithmetic and copies ran while one was open for 0% of the time, Pallas kernels for 0%

commit v1 on v0

v1 whole, which is shorter than its diff:
```python
import jax
import jax.numpy as jnp
from jax import lax
from jax.experimental import pallas as pl
from jax.experimental.pallas import tpu as pltpu
from jax.sharding import PartitionSpec as P

S = 512
D = 1024
G = 256
HALF = 256
BF = jnp.bfloat16
F32 = jnp.float32
LOG2E = 1.4426950408889634
VSCALE = 2.0**-14
SQRT_HALF = 0.7071067811865476
MESH = pl.DeviceIdType.MESH
ARRAYS = ("qkv", "out", "up", "down")


def dot(a, b):
    return jnp.dot(a, b, preferred_element_type=F32)


def norm_rows(x, gain):
    mean = jnp.mean(x, axis=-1, keepdims=True)
    centered = x - mean
    variance = jnp.mean(centered * centered, axis=-1, keepdims=True)
    return centered * lax.rsqrt(variance + 1e-12) * gain


def gelu(u):
    return 0.5 * u * (1.0 + lax.erf(u * SQRT_HALF))


class Sems:
    def __init__(self, send, recv):
        self.send, self.recv, self.used = send, recv, 0

    def remote(self, src, dst, device):
        i = self.used
        self.used += 1
        return pltpu.make_async_remote_copy(
            src_ref=src, dst_ref=dst, send_sem=self.send.at[i], recv_sem=self.recv.at[i], device_id=device, device_id_type=MESH
        )


N_SEMS = 36


def kernel(
    states_q, states_d, qlen, dlen, order, w_qkv, w_out, w_up, w_down, gain_attn, gain_mlp,
    out_q, out_d, out_loss,
    b_qkv, b_out, b_up, b_down, h, hout, qkv, qm, km, kt, vm, cf, ctx, acc, mixed, act, qtab, dtab, tile,
    send, recv, local, h_send, h_recv, t1_send, t1_recv, t2_send, t2_recv, t3_send, t3_recv,
):
    dp, pipe, z = lax.axis_index("dp"), lax.axis_index("pipe"), lax.axis_index("tensor")
    core = lax.rem(dp, 2)
    first = 1 - (pipe + 3) // 4

    def at(dp_=dp, pipe_=pipe, z_=z):
        return (dp_, pipe_, z_)

    up_z, down_z = at(z_=lax.rem(z + 1, 4)), at(z_=lax.rem(z + 3, 4))
    sibling = at(dp_=dp + 1 - 2 * core)

    barrier = pltpu.get_barrier_semaphore()
    for k in range(1, 8):
        pl.semaphore_signal(barrier, inc=1, device_id=at(dp_=lax.rem(dp + k, 8)), device_id_type=MESH)
    for k in range(1, 4):
        pl.semaphore_signal(barrier, inc=1, device_id=at(pipe_=lax.rem(pipe + k, 4)), device_id_type=MESH)
        pl.semaphore_signal(barrier, inc=1, device_id=at(z_=lax.rem(z + k, 4)), device_id_type=MESH)

    own = {"qkv": w_qkv, "out": w_out, "up": w_up, "down": w_down}
    full = {"qkv": b_qkv, "out": b_out, "up": b_up, "down": b_down}
    depth = {"qkv": 1024, "out": 256, "up": 1024, "down": 1024}

    def rows_of(name, ref, which):
        n = depth[name] // 4
        if which == "a":
            start, size = core * 2 * n, n
        elif which == "b":
            start, size = core * 2 * n + n, n
        elif which == "all":
            start, size = core * 2 * n, 2 * n
        else:
            start, size = (1 - core) * 2 * n, 2 * n
        sl = pl.ds(pl.multiple_of(start, n), size)
        return ref.at[:, sl, :] if name == "qkv" else ref.at[sl, :]

    sems = Sems(send, recv)
    hop1, hop2, d2d = {}, {}, {}
    for name in ARRAYS:
        for part in ("a", "b"):
            src = rows_of(name, own[name].at[0], part)
            hop1[name, 1, part] = sems.remote(src, rows_of(name, full[name].at[1], part), up_z)
            hop1[name, 2, part] = sems.remote(src, rows_of(name, full[name].at[2], part), down_z)
        hop2[name, "a"] = sems.remote(rows_of(name, full[name].at[1], "a"), rows_of(name, full[name].at[3], "a"), up_z)
        hop2[name, "b"] = sems.remote(rows_of(name, full[name].at[2], "b"), rows_of(name, full[name].at[3], "b"), down_z)
        for slot in (1, 2, 3):
            mine = rows_of(name, full[name].at[slot], "all")
            d2d[name, slot] = sems.remote(mine, mine, sibling)
    loads = {name: pltpu.make_async_copy(own[name].at[0], full[name].at[0], local.at[i]) for i, name in enumerate(ARRAYS)}

    def start_own(names):
        for name in names:
            for part in ("a", "b"):
                hop1[name, 1, "a" if part == "a" else "b"].start()
                hop1[name, 2, "b" if part == "a" else "a"].start()

    def forward(names):
        for name in names:
            hop1[name, 1, "a"].wait_recv()
            hop2[name, "a"].start()
            hop1[name, 2, "b"].wait_recv()
            hop2[name, "b"].start()

    def near(names):
        for name in names:
            hop1[name, 1, "b"].wait_recv()
            d2d[name, 1].start()
            hop1[name, 2, "a"].wait_recv()
            d2d[name, 2].start()
        for name in names:
            for slot in (1, 2):
                d2d[name, slot].wait_recv()

    def far(names):
        for name in names:
            hop2[name, "a"].wait_recv()
            hop2[name, "b"].wait_recv()
            d2d[name, 3].start()
        for name in names:
            d2d[name, 3].wait_recv()

    for name in ARRAYS:
        loads[name].start()
    gains = [pltpu.make_async_copy(gain_attn, tile.at[pl.ds(0, 1)], local.at[4]), pltpu.make_async_copy(gain_mlp, tile.at[pl.ds(8, 1)], local.at[5])]
    for g in gains:
        g.start()

    pl.semaphore_wait(barrier, 13)
    ATT, MLP = ("qkv", "out"), ("up", "down")
    start_own(ATT)

    z_low = lax.rem(z, 2)

    @pl.when((first == 1) & (z < 2))
    def _():
        c = pltpu.make_async_copy(states_q.at[z_low], h, local.at[6])
        c.start()
        c.wait()

    @pl.when((first == 1) & (z >= 2))
    def _():
        c = pltpu.make_async_copy(states_d.at[z_low], h, local.at[6])
        c.start()
        c.wait()

    @pl.when(first == 0)
    def _():
        forward(ATT)
        start_own(MLP)
        near(ATT)
        far(ATT)
        forward(MLP)
        near(MLP)
        far(MLP)

    for name in ARRAYS:
        loads[name].wait()
    for g in gains:
        g.wait()

    nblk = S // HALF

    def hop_x(r):
        rows = pl.ds(r * HALF, HALF)
        return pltpu.make_async_remote_copy(
            src_ref=hout.at[rows], dst_ref=h.at[rows], send_sem=h_send.at[r], recv_sem=h_recv.at[r],
            device_id=at(pipe_=lax.rem(pipe + 1, 4)), device_id_type=MESH,
        )

    @pl.when(first == 0)
    def _():
        for r in range(nblk):
            hop_x(r).wait_recv()

    length = jnp.where(z == 0, qlen[0], jnp.where(z == 1, qlen[1], jnp.where(z == 2, dlen[0], dlen[1])))
    lane = lax.broadcasted_iota(jnp.int32, (1, G), 1)
    head = lane // 64
    bias = jnp.where(lax.broadcasted_iota(jnp.int32, (1, S), 1) < length, 0.0, -1e30).astype(BF)
    krow = lax.broadcasted_iota(jnp.int32, (G, 1), 0)
    one, zero = jnp.ones((), BF), jnp.zeros((), BF)

    @pl.loop(0, 4)
    def _(j):
        @pl.when((first == 1) & (j == 1))
        def _():
            forward(ATT)
            start_own(MLP)
            near(ATT)

        @pl.when((first == 1) & (j == 3))
        def _():
            far(ATT)

        @pl.loop(0, 3)
        def _(i):
            scale = jnp.where(i == 0, 0.125 * LOG2E, jnp.where(i == 2, VSCALE, 1.0)).astype(F32)
            qkv[i] = (dot(h[...], b_qkv[j, i]) * scale).astype(BF)

        kt[...] = qkv[1].T
        for hd in range(4):
            nxt = (hd + 1) % 4
            mine, other, mark = head == hd, head == nxt, lane == nxt * 64
            qm[hd] = jnp.where(mine, qkv[0], jnp.where(mark, one, zero))
            km[hd] = jnp.where(krow == nxt * 64, bias, kt[...])
            vm[hd] = jnp.where(mine, qkv[2], jnp.where(other, one, zero))
        for hd in range(4):
            mine = head == hd
            for r in range(2):
                rows = slice(r * 256, (r + 1) * 256)
                p = jnp.exp2(dot(qm[hd, rows, :], km[hd])).astype(BF)
                o = dot(p, vm[hd])
                total = pltpu.roll(o, 192, 1)
                t = jnp.where(total > 2.0**60, 2.0**-64, 1.0).astype(F32)
                c = (o * t) * (1.0 / (total * t)) * (1.0 / VSCALE)
                cf[rows, :] = jnp.where(mine, c, cf[rows, :] if hd else c)
        ctx[:, pl.ds(pl.multiple_of(j * G, G), G)] = cf[...].astype(BF)

    @pl.loop(0, 4)
    def _(n):
        cs = pl.ds(pl.multiple_of(n * 256, 256), 256)
        acc[:, cs] = sum(dot(ctx[:, j * G : (j + 1) * G], b_out[j, :, cs]) for j in range(4))

    @pl.loop(0, 4)
    def _(r):
        for q in range(4):
            rows = pl.ds(pl.multiple_of(r * 128 + q * 32, 32), 32)
            mixed[rows, :] = norm_rows(h[rows, :].astype(F32) + acc[rows, :], tile[0:1, :]).astype(BF)

    @pl.loop(0, 4 * nblk)
    def _(i):
        j = first * (i // nblk) + (1 - first) * lax.rem(i, 4)
        r = first * lax.rem(i, nblk) + (1 - first) * (i // 4)

        @pl.when((first == 1) & (i == nblk))
        def _():
            forward(MLP)
            near(MLP)

        @pl.when((first == 1) & (i == 3 * nblk))
        def _():
            far(MLP)

        rows = pl.ds(pl.multiple_of(r * HALF, HALF), HALF)

        @pl.loop(0, 4)
        def _(n):
            cs = pl.ds(pl.multiple_of(n * 256, 256), 256)
            act[:, cs] = gelu(dot(mixed[rows, :], b_up[j, :, cs])).astype(BF)

        @pl.loop(0, 4)
        def _(n):
            cs = pl.ds(pl.multiple_of(n * 256, 256), 256)
            part = dot(act[...], b_down[j, :, cs])
            acc[rows, cs] = jnp.where(j == 0, part, acc[rows, cs] + part)

        @pl.when(j == 3)
        def _():
            @pl.loop(0, HALF // 64)
            def _(q):
                for u in range(2):
                    rr = pl.ds(pl.multiple_of(r * HALF + q * 64 + u * 32, 32), 32)
                    hout[rr, :] = norm_rows(mixed[rr, :].astype(F32) + acc[rr, :], tile[8:9, :]).astype(BF)

            for rs in range(nblk):

                @pl.when((pipe < 3) & (r == rs))
                def _():
                    hop_x(rs).start()

    def t1(k):
        return pltpu.make_async_remote_copy(
            src_ref=dtab.at[z_low, dp], dst_ref=dtab.at[z_low, dp], send_sem=t1_send.at[k - 1], recv_sem=t1_recv.at[k - 1],
            device_id=at(dp_=lax.rem(dp + k, 8)), device_id_type=MESH,
        )

    def t1_in(k):
        there = lax.rem(dp + 8 - k, 8)
        return pltpu.make_async_remote_copy(
            src_ref=dtab.at[z_low, there], dst_ref=dtab.at[z_low, there], send_sem=t1_send.at[k - 1], recv_sem=t1_recv.at[k - 1],
            device_id=at(dp_=lax.rem(dp + k, 8)), device_id_type=MESH,
        )

    def t2(tab, slot, k):
        return pltpu.make_async_remote_copy(
            src_ref=tab.at[slot], dst_ref=tab.at[slot], send_sem=t2_send.at[k - 1], recv_sem=t2_recv.at[k - 1],
            device_id=at(z_=lax.rem(z + k, 4)), device_id_type=MESH,
        )

    def t3(tab, i, k):
        return pltpu.make_async_remote_copy(
            src_ref=tab, dst_ref=tab, send_sem=t3_send.at[i, k], recv_sem=t3_recv.at[i], device_id=at(pipe_=k), device_id_type=MESH
        )

    @pl.when(pipe < 3)
    def _():
        t3(qtab, 0, 0).wait_recv()
        t3(dtab, 1, 0).wait_recv()

    @pl.when(pipe == 3)
    def _():
        acc[0:8, :] = jnp.zeros((8, D), F32)

        @pl.loop(0, 16)
        def _(r):
            rows = pl.ds(pl.multiple_of(r * 32, 32), 32)
            keep = lax.broadcasted_iota(jnp.int32, (32, 1), 0) + r * 32 < length
            x = jnp.where(keep, hout[rows, :].astype(F32), 0.0)
            acc[0:8, :] += x[0:8] + x[8:16] + x[16:24] + x[24:32]

        pooled = jnp.sum(acc[0:8, :], axis=0, keepdims=True) / length.astype(F32)
        emb = pooled * lax.rsqrt(jnp.sum(pooled * pooled, axis=-1, keepdims=True) + 1e-6)
        emb = emb.astype(BF).astype(F32)

        @pl.when(z < 2)
        def _():
            for k in range(8):
                qtab[z_low, k : k + 1, :] = emb[:, k * 128 : (k + 1) * 128]

        @pl.when(z >= 2)
        def _():
            for k in range(8):
                dtab[z_low, dp, k : k + 1, :] = emb[:, k * 128 : (k + 1) * 128]
            for k in range(1, 8):
                t1(k).start()
            for k in range(1, 8):
                t1_in(k).wait_recv()
            for k in range(1, 4):
                t2(dtab, z_low, k).start()

        @pl.when(z < 2)
        def _():
            for k in range(1, 4):
                t2(qtab, z_low, k).start()

        for k in range(1, 4):
            there = lax.rem(z + 4 - k, 4)

            @pl.when(there < 2)
            def _():
                t2(qtab, lax.rem(there, 2), k).wait_recv()

            @pl.when(there >= 2)
            def _():
                t2(dtab, lax.rem(there, 2), k).wait_recv()

        for k in range(3):
            t3(qtab, 0, k).start()
            t3(dtab, 1, k).start()

    doc_dp = lax.broadcasted_iota(jnp.int32, (8, 1), 0)
    for i in range(2):
        total, positive = jnp.zeros((1, 1), F32), jnp.zeros((1, 1), F32)
        for s in range(2):
            prod = dtab[s] * qtab[i][None]
            score = jnp.sum(jnp.sum(prod, axis=1), axis=1, keepdims=True) / 0.05
            total += jnp.sum(jnp.exp(score), axis=0, keepdims=True)
            hit = (doc_dp == dp) & (order[0, i] == s)
            positive += jnp.sum(jnp.where(hit, score, 0.0), axis=0, keepdims=True)
        out_loss[i : i + 1, :] = jnp.broadcast_to(jnp.log(total) - positive, (1, 128))
    piece = pipe * 4 + z
    row, side = piece // 2, lax.rem(piece, 2)
    for i in range(2):
        qrow = qtab[i, pl.ds(row, 1), :]
        out_q[i : i + 1, :] = jnp.where(side == 0, qrow, pltpu.roll(qrow, 64, 1))[:, :64].astype(BF)
        drow = dtab[i, dp, pl.ds(row, 1), :]
        out_d[i : i + 1, :] = jnp.where(side == 0, drow, pltpu.roll(drow, 64, 1))[:, :64].astype(BF)

    for copy in [*hop1.values(), *hop2.values(), *d2d.values()]:
        copy.wait_send()

    @pl.when(pipe < 3)
    def _():
        for r in range(nblk):
            hop_x(r).wait_send()

    @pl.when(pipe == 3)
    def _():
        for k in range(3):
            t3(qtab, 0, k).wait_send()
            t3(dtab, 1, k).wait_send()

        @pl.when(z >= 2)
        def _():
            for k in range(1, 8):
                t1(k).wait_send()
            for k in range(1, 4):
                t2(dtab, z_low, k).wait_send()

        @pl.when(z < 2)
        def _():
            for k in range(1, 4):
                t2(qtab, z_low, k).wait_send()


def per_device(query_states, doc_states, query_len, doc_len, doc_order, w_qkv, w_out, w_up, w_down, gain_attn, gain_mlp):
    anyspace = pl.BlockSpec(memory_space=pl.ANY)
    smem = pl.BlockSpec(memory_space=pltpu.SMEM)
    vmem = pl.BlockSpec(memory_space=pltpu.VMEM)
    q, d, loss = pl.pallas_call(
        kernel,
        out_shape=(jax.ShapeDtypeStruct((2, 64), BF), jax.ShapeDtypeStruct((2, 64), BF), jax.ShapeDtypeStruct((2, 128), F32)),
        in_specs=[anyspace, anyspace, smem, smem, smem, *[anyspace] * 6],
        out_specs=(vmem, vmem, vmem),
        scratch_shapes=[
            pltpu.VMEM((4, 3, D, G), BF),
            pltpu.VMEM((4, G, D), BF),
            pltpu.VMEM((4, D, D), BF),
            pltpu.VMEM((4, D, D), BF),
            pltpu.VMEM((S, D), BF),
            pltpu.VMEM((S, D), BF),
            pltpu.VMEM((3, S, G), BF),
            pltpu.VMEM((4, S, G), BF),
            pltpu.VMEM((4, G, S), BF),
            pltpu.VMEM((G, S), BF),
            pltpu.VMEM((4, S, G), BF),
            pltpu.VMEM((S, G), F32),
            pltpu.VMEM((S, D), BF),
            pltpu.VMEM((S, D), F32),
            pltpu.VMEM((S, D), BF),
            pltpu.VMEM((HALF, D), BF),
            pltpu.VMEM((2, 8, 128), F32),
            pltpu.VMEM((2, 8, 8, 128), F32),
            pltpu.VMEM((16, D), F32),
            pltpu.SemaphoreType.DMA((N_SEMS,)),
            pltpu.SemaphoreType.DMA((N_SEMS,)),
            pltpu.SemaphoreType.DMA((8,)),
            pltpu.SemaphoreType.DMA((S // HALF,)),
            pltpu.SemaphoreType.DMA((S // HALF,)),
            pltpu.SemaphoreType.DMA((7,)),
            pltpu.SemaphoreType.DMA((7,)),
            pltpu.SemaphoreType.DMA((3,)),
            pltpu.SemaphoreType.DMA((3,)),
            pltpu.SemaphoreType.DMA((2, 3)),
            pltpu.SemaphoreType.DMA((2,)),
        ],
        compiler_params=pltpu.CompilerParams(collective_id=0, has_side_effects=True, vmem_limit_bytes=63 * 2**20),
        name="encode",
    )(query_states, doc_states, query_len, doc_len, doc_order, w_qkv, w_out, w_up, w_down, gain_attn, gain_mlp)
    return q, d, loss[:, 0]


def solution(mesh):
    in_specs = (
        P("dp", None, None),
        P("dp", None, None),
        P("dp"),
        P("dp"),
        P("dp", None),
        P("pipe", None, None, "tensor"),
        P("pipe", "tensor", None),
        P("pipe", None, "tensor"),
        P("pipe", "tensor", None),
        P("pipe", None),
        P("pipe", None),
    )
    out_specs = (P("dp", ("pipe", "tensor")), P("dp", ("pipe", "tensor")), P("dp"))
    return jax.shard_map(per_device, mesh=mesh, in_specs=in_specs, out_specs=out_specs, check_vma=False)
```

time: 659 us -> 296 us (0.45)
  waiting for transfers between devices: 376 us -> 0 us
  Pallas kernels: 0 us -> 292 us
  matrix products: 173 us -> 0 us
  starting transfers between devices: 29.6 us -> 0 us
  local copies, waits for them, and re-layouts: 26.4 us -> 3.55 us
  other arithmetic: 22.3 us -> 0 us
  between operations: 14.6 us -> 0.64 us
  blocking collectives: 13.3 us -> 0 us
    pallas_call x0 -> x1, Pallas kernels: none -> 292 us  [per_device(): pl.pallas_call(kernel, out_shape=(jax.ShapeDtypeStruct((2, 64), BF), jax....]
    all_gather x4 -> x0, waiting for transfers between devices: 274 us -> none  [the longest x1 85.6 us: per_device(): lax.all_gather(w_down, 'tensor', axis=1, tiled=True)]
    dot_general x33 -> x0, matrix products: 173 us -> none  [the longest x4 90.3 us: encode_layer(): upward = jnp.dot(mixed, w_up, preferred_element_type=jnp.float32)]
    ppermute x4 -> x0, waiting for transfers between devices: 80.8 us -> none  [from_behind(): lax.ppermute(value, axis, [(source, source + steps) for source in range(i...]
    all_to_all x3 -> x0, waiting for transfers between devices: 18.1 us -> none  [the longest x2 12.9 us: copy_for_each(): lax.all_to_all(jnp.broadcast_to(x[None], (peers, *x.shape)), axis, 0, 0,...]
    convert_element_type x12 -> x0, local copies, waits for them, and re-layouts: 17.2 us -> none  [the longest x4 9.06 us: encode_layer(): jnp.dot(hidden, w_qkv[2], preferred_element_type=jnp.float32)]
    ppermute x4 -> x0, starting transfers between devices: 16.8 us -> none  [from_behind(): lax.ppermute(value, axis, [(source, source + steps) for source in range(i...]
    all_gather x1 -> x0, blocking collectives: 13.3 us -> none  [from_root(): lax.all_gather(x, axis)]
  transfers between devices with their start and end apart: 11 -> 0, of which waited for: 11 -> 0; matrix products, arithmetic and copies ran while one was open for 0% -> 0% of each run, Pallas kernels for 0% -> 0%
where the time goes in v1:
time: 296 us
  Pallas kernels  292 us (99%)
  local copies, waits for them, and re-layouts  3.55 us (1%)
    pallas_call x1, Pallas kernels, per_device(): pl.pallas_call(kernel, out_shape=(jax.ShapeDtypeStruct((2, 64), BF), jax....  292 us

profile of v1, /device:TPU:0, one launch (start us, length us, event | category | flops | bytes accessed | tf_op | source)
XLA Modules:
  0.0 296.2 jit_solution(14124584755488852035)
XLA Ops:
  0.6 292.0 %encode.1 = (bf16[2,64]{1,0:T(2,128)(2,1)}, bf16[2,64]{1,0:T(2,128)(2,1)}, f32[2,128]{1,0:T(2,128)}) custom-call(bf16[2,512,1024]{2,1,0:T(8,128)(2,1)} %states_q.1, bf16[2,512,1024]{2,1,0:T(8,128)(2,1)} %states_d.1, s32[2]{0:T(128)} %qlen.1, s32[2]{0:T(128)} %dlen.1, s32[1,2]{1,0:T(1,128)} %order.1, bf16[1,3,1024,256]{3,2,1,0:T(8,128)(2,1)} %w_qkv.1, ...), custom_call_target="tpu_custom_call" | custom-call | tf_op jit(solution)/shard_map/encode/pallas_call | solution.py:413
  292.7 1.3 slice_reduce_fusion
  294.0 1.1 copy.16
  295.1 1.1 copy.17

commit v2 on v1

--- a/solution.py
+++ b/solution.py
@@ -16,6 +16,8 @@
 SQRT_HALF = 0.7071067811865476
 MESH = pl.DeviceIdType.MESH
 ARRAYS = ("qkv", "out", "up", "down")
+MLP = ("up", "down")
+depth_half = {"qkv": 512, "out": 128, "up": 512, "down": 512}
 
 
 def dot(a, b):
@@ -45,14 +47,20 @@
         )
 
 
-N_SEMS = 36
+    def again(self, i, ref, device):
+        return pltpu.make_async_remote_copy(
+            src_ref=ref, dst_ref=ref, send_sem=self.send.at[i], recv_sem=self.recv.at[i], device_id=device, device_id_type=MESH
+        )
+
+
+N_SEMS = 60
 
 
 def kernel(
     states_q, states_d, qlen, dlen, order, w_qkv, w_out, w_up, w_down, gain_attn, gain_mlp,
     out_q, out_d, out_loss,
     b_qkv, b_out, b_up, b_down, h, hout, qkv, qm, km, kt, vm, cf, ctx, acc, mixed, act, qtab, dtab, tile,
-    send, recv, local, h_send, h_recv, t1_send, t1_recv, t2_send, t2_recv, t3_send, t3_recv,
+    send, recv, local, c_send, c_recv, h_send, h_recv, t1_send, t1_recv, t2_send, t2_recv, t3_send, t3_recv,
 ):
     dp, pipe, z = lax.axis_index("dp"), lax.axis_index("pipe"), lax.axis_index("tensor")
     core = lax.rem(dp, 2)
@@ -71,67 +79,147 @@
         pl.semaphore_signal(barrier, inc=1, device_id=at(pipe_=lax.rem(pipe + k, 4)), device_id_type=MESH)
         pl.semaphore_signal(barrier, inc=1, device_id=at(z_=lax.rem(z + k, 4)), device_id_type=MESH)
 
+    y = dp // 2
     own = {"qkv": w_qkv, "out": w_out, "up": w_up, "down": w_down}
     full = {"qkv": b_qkv, "out": b_out, "up": b_up, "down": b_down}
-    depth = {"qkv": 1024, "out": 256, "up": 1024, "down": 1024}
-
-    def rows_of(name, ref, which):
-        n = depth[name] // 4
-        if which == "a":
-            start, size = core * 2 * n, n
-        elif which == "b":
-            start, size = core * 2 * n + n, n
-        elif which == "all":
-            start, size = core * 2 * n, 2 * n
-        else:
-            start, size = (1 - core) * 2 * n, 2 * n
-        sl = pl.ds(pl.multiple_of(start, n), size)
+    north, south = at(dp_=lax.rem(dp + 2, 8)), at(dp_=lax.rem(dp + 6, 8))
+
+    def window(name, ref, start, size):
+        sl = pl.ds(pl.multiple_of(start, 16), size)
         return ref.at[:, sl, :] if name == "qkv" else ref.at[sl, :]
 
+    def quarter(k):
+        return core * 512 + 128 + 96 * lax.rem(y + k + 4, 4)
+
+    parts = {
+        "qkv": {"Z": (core * 512, 512)},
+        "out": {"Z": (core * 128, 128)},
+        "up": {"Z": (core * 512, 128), "Q": (quarter(0), 96)},
+        "down": {"Z": (core * 512, 128), "Q": (quarter(0), 96)},
+    }
     sems = Sems(send, recv)
-    hop1, hop2, d2d = {}, {}, {}
+    hop1, hop2, yhop1, yin1, yhop2, yin2, d2d = {}, {}, {}, {}, {}, {}, {}
     for name in ARRAYS:
-        for part in ("a", "b"):
-            src = rows_of(name, own[name].at[0], part)
-            hop1[name, 1, part] = sems.remote(src, rows_of(name, full[name].at[1], part), up_z)
-            hop1[name, 2, part] = sems.remote(src, rows_of(name, full[name].at[2], part), down_z)
-        hop2[name, "a"] = sems.remote(rows_of(name, full[name].at[1], "a"), rows_of(name, full[name].at[3], "a"), up_z)
-        hop2[name, "b"] = sems.remote(rows_of(name, full[name].at[2], "b"), rows_of(name, full[name].at[3], "b"), down_z)
+        buf = full[name]
+        for part, (start, size) in parts[name].items():
+            src = window(name, own[name].at[0], start, size)
+            hop1[name, part, 1] = sems.remote(src, window(name, buf.at[1], start, size), up_z)
+            hop1[name, part, 2] = sems.remote(src, window(name, buf.at[2], start, size), down_z)
+            half = size // 2
+            a, b = (start, half), (start + half, half)
+            hop2[name, part, "a"] = sems.remote(window(name, buf.at[1], *a), window(name, buf.at[3], *a), up_z)
+            hop2[name, part, "b"] = sems.remote(window(name, buf.at[2], *b), window(name, buf.at[3], *b), down_z)
         for slot in (1, 2, 3):
-            mine = rows_of(name, full[name].at[slot], "all")
+            size = depth_half[name]
+            mine = window(name, buf.at[slot], core * size, size)
             d2d[name, slot] = sems.remote(mine, mine, sibling)
+    for name in MLP:
+        for slot in (1, 2, 3):
+            buf = full[name].at[slot]
+
+            def part(k, first_row=0, size=96, buf=buf, name=name):
+                return window(name, buf, quarter(k) + first_row, size)
+
+            for sign, to in ((1, north), (-1, south)):
+                i = sems.used
+                yhop1[name, slot, sign] = sems.remote(part(0), part(0), to)
+                yin1[name, slot, sign] = sems.again(i, part(-sign), to)
+                row = 0 if sign == 1 else 48
+                i = sems.used
+                yhop2[name, slot, sign] = sems.remote(part(-sign, row, 48), part(-sign, row, 48), to)
+                yin2[name, slot, sign] = sems.again(i, part(2, row, 48), to)
     loads = {name: pltpu.make_async_copy(own[name].at[0], full[name].at[0], local.at[i]) for i, name in enumerate(ARRAYS)}
 
-    def start_own(names):
-        for name in names:
-            for part in ("a", "b"):
-                hop1[name, 1, "a" if part == "a" else "b"].start()
-                hop1[name, 2, "b" if part == "a" else "a"].start()
-
-    def forward(names):
-        for name in names:
-            hop1[name, 1, "a"].wait_recv()
-            hop2[name, "a"].start()
-            hop1[name, 2, "b"].wait_recv()
-            hop2[name, "b"].start()
-
-    def near(names):
-        for name in names:
-            hop1[name, 1, "b"].wait_recv()
-            d2d[name, 1].start()
-            hop1[name, 2, "a"].wait_recv()
-            d2d[name, 2].start()
-        for name in names:
-            for slot in (1, 2):
-                d2d[name, slot].wait_recv()
-
-    def far(names):
-        for name in names:
-            hop2[name, "a"].wait_recv()
-            hop2[name, "b"].wait_recv()
-            d2d[name, 3].start()
-        for name in names:
-            d2d[name, 3].wait_recv()
+    def begin(name, part):
+        hop1[name, part, 1].start()
+        hop1[name, part, 2].start()
+
+    def z_near(name, part):
+        hop1[name, part, 1].wait_recv()
+        hop2[name, part, "a"].start()
+        hop1[name, part, 2].wait_recv()
+        hop2[name, part, "b"].start()
+
+    def z_far(name, part):
+        hop2[name, part, "a"].wait_recv()
+        hop2[name, part, "b"].wait_recv()
+
+    def y_begin(name, *slots):
+        for slot in slots:
+            for sign in (1, -1):
+                yhop1[name, slot, sign].start()
+
+    def y_on(name, *slots):
+        for slot in slots:
+            for sign in (1, -1):
+                yin1[name, slot, sign].wait_recv()
+                yhop2[name, slot, sign].start()
+
+    def y_end(name, *slots):
+        for slot in slots:
+            for sign in (1, -1):
+                yin2[name, slot, sign].wait_recv()
+            d2d[name, slot].start()
+
+    def arrive(name, *slots):
+        for slot in slots:
+            d2d[name, slot].wait_recv()
+
+    def give(name, *slots):
+        for slot in slots:
+            d2d[name, slot].start()
+
+    def begin_all():
+        begin("up", "Q")
+        begin("down", "Q")
+
+    def step1():
+        z_near("up", "Q")
+        y_begin("up", 1, 2)
+
+    def step2():
+        begin("out", "Z")
+        z_near("down", "Q")
+        y_begin("down", 1, 2)
+
+    def step3():
+        begin("up", "Z")
+        begin("down", "Z")
+        z_far("up", "Q")
+        y_begin("up", 3)
+
+    def step4():
+        z_far("down", "Q")
+        y_begin("down", 3)
+        z_near("out", "Z")
+        give("out", 1, 2)
+        y_on("up", 1, 2)
+
+    def step5():
+        z_near("up", "Z")
+        z_far("out", "Z")
+        give("out", 3)
+        arrive("out", 1, 2, 3)
+
+    def step6():
+        y_on("down", 1, 2)
+        z_near("down", "Z")
+
+    def step7():
+        y_on("up", 3)
+        y_end("up", 1, 2)
+        y_on("down", 3)
+        y_end("down", 1, 2)
+        arrive("up", 1, 2)
+        arrive("down", 1, 2)
+
+    def step8():
+        z_far("up", "Z")
+        y_end("up", 3)
+        z_far("down", "Z")
+        y_end("down", 3)
+        arrive("up", 3)
+        arrive("down", 3)
 
     for name in ARRAYS:
         loads[name].start()
@@ -139,45 +227,65 @@
     for g in gains:
         g.start()
 
+    def input_copy(ref, index, k):
+        return pltpu.make_async_copy(ref.at[index], h.at[k], local.at[8 + k])
+
+    @pl.when(first == 1)
+    def _():
+        for k in range(4):
+            seq = lax.rem(z + k, 4)
+
+            @pl.when(seq < 2)
+            def _():
+                input_copy(states_q, lax.rem(seq, 2), k).start()
+
+            @pl.when(seq >= 2)
+            def _():
+                input_copy(states_d, lax.rem(seq, 2), k).start()
+
     pl.semaphore_wait(barrier, 13)
-    ATT, MLP = ("qkv", "out"), ("up", "down")
-    start_own(ATT)
-
+    begin_all()
     z_low = lax.rem(z, 2)
 
-    @pl.when((first == 1) & (z < 2))
-    def _():
-        c = pltpu.make_async_copy(states_q.at[z_low], h, local.at[6])
-        c.start()
-        c.wait()
-
-    @pl.when((first == 1) & (z >= 2))
-    def _():
-        c = pltpu.make_async_copy(states_d.at[z_low], h, local.at[6])
-        c.start()
-        c.wait()
-
     @pl.when(first == 0)
     def _():
-        forward(ATT)
-        start_own(MLP)
-        near(ATT)
-        far(ATT)
-        forward(MLP)
-        near(MLP)
-        far(MLP)
+        step1()
+        begin("qkv", "Z")
+        step2()
+        step3()
+        z_near("qkv", "Z")
+        give("qkv", 1, 2)
+        step4()
+        step5()
+        step6()
+        z_far("qkv", "Z")
+        give("qkv", 3)
+        step7()
+        step8()
+        arrive("qkv", 1, 2, 3)
 
     for name in ARRAYS:
         loads[name].wait()
     for g in gains:
         g.wait()
 
+    @pl.when(first == 1)
+    def _():
+        for k in range(4):
+            input_copy(states_q, 0, k).wait()
+
+    def share(k):
+        return pltpu.make_async_remote_copy(
+            src_ref=ctx.at[4 + k], dst_ref=ctx.at[(0, 1, 3, 2)[k]], send_sem=c_send.at[k - 1], recv_sem=c_recv.at[k - 1],
+            device_id=at(z_=lax.rem(z + k, 4)), device_id_type=MESH,
+        )
+
     nblk = S // HALF
 
     def hop_x(r):
         rows = pl.ds(r * HALF, HALF)
         return pltpu.make_async_remote_copy(
-            src_ref=hout.at[rows], dst_ref=h.at[rows], send_sem=h_send.at[r], recv_sem=h_recv.at[r],
+            src_ref=hout.at[rows], dst_ref=h.at[0, rows], send_sem=h_send.at[r], recv_sem=h_recv.at[r],
             device_id=at(pipe_=lax.rem(pipe + 1, 4)), device_id_type=MESH,
         )
 
@@ -186,29 +294,40 @@
         for r in range(nblk):
             hop_x(r).wait_recv()
 
-    length = jnp.where(z == 0, qlen[0], jnp.where(z == 1, qlen[1], jnp.where(z == 2, dlen[0], dlen[1])))
+    def length_of(seq):
+        return jnp.where(seq == 0, qlen[0], jnp.where(seq == 1, qlen[1], jnp.where(seq == 2, dlen[0], dlen[1])))
+
+    length = length_of(z)
     lane = lax.broadcasted_iota(jnp.int32, (1, G), 1)
     head = lane // 64
-    bias = jnp.where(lax.broadcasted_iota(jnp.int32, (1, S), 1) < length, 0.0, -1e30).astype(BF)
     krow = lax.broadcasted_iota(jnp.int32, (G, 1), 0)
     one, zero = jnp.ones((), BF), jnp.zeros((), BF)
 
     @pl.loop(0, 4)
     def _(j):
+        ahead = first * lax.rem(j + 1, 4)
+        group = (1 - first) * j
+        bias = jnp.where(lax.broadcasted_iota(jnp.int32, (1, S), 1) < length_of(lax.rem(z + ahead, 4)), 0.0, -1e30).astype(BF)
+
         @pl.when((first == 1) & (j == 1))
         def _():
-            forward(ATT)
-            start_own(MLP)
-            near(ATT)
+            share(1).start()
+            step1()
+
+        @pl.when((first == 1) & (j == 2))
+        def _():
+            share(2).start()
+            step2()
 
         @pl.when((first == 1) & (j == 3))
         def _():
-            far(ATT)
+            share(3).start()
+            step3()
 
         @pl.loop(0, 3)
         def _(i):
             scale = jnp.where(i == 0, 0.125 * LOG2E, jnp.where(i == 2, VSCALE, 1.0)).astype(F32)
-            qkv[i] = (dot(h[...], b_qkv[j, i]) * scale).astype(BF)
+            qkv[i] = (dot(h[ahead], b_qkv[group, i]) * scale).astype(BF)
 
         kt[...] = qkv[1].T
         for hd in range(4):
@@ -227,32 +346,42 @@
                 t = jnp.where(total > 2.0**60, 2.0**-64, 1.0).astype(F32)
                 c = (o * t) * (1.0 / (total * t)) * (1.0 / VSCALE)
                 cf[rows, :] = jnp.where(mine, c, cf[rows, :] if hd else c)
-        ctx[:, pl.ds(pl.multiple_of(j * G, G), G)] = cf[...].astype(BF)
+        ctx[group + ahead + 4 * ((ahead + 3) // 4)] = cf[...].astype(BF)
+
+    @pl.when(first == 1)
+    def _():
+        step4()
+        step5()
+        for k in range(1, 4):
+            share(k).wait_recv()
 
     @pl.loop(0, 4)
     def _(n):
         cs = pl.ds(pl.multiple_of(n * 256, 256), 256)
-        acc[:, cs] = sum(dot(ctx[:, j * G : (j + 1) * G], b_out[j, :, cs]) for j in range(4))
+        acc[:, cs] = sum(dot(ctx[j], b_out[j, :, cs]) for j in range(4))
 
     @pl.loop(0, 4)
     def _(r):
         for q in range(4):
             rows = pl.ds(pl.multiple_of(r * 128 + q * 32, 32), 32)
-            mixed[rows, :] = norm_rows(h[rows, :].astype(F32) + acc[rows, :], tile[0:1, :]).astype(BF)
+            mixed[rows, :] = norm_rows(h[0, rows, :].astype(F32) + acc[rows, :], tile[0:1, :]).astype(BF)
 
     @pl.loop(0, 4 * nblk)
     def _(i):
         j = first * (i // nblk) + (1 - first) * lax.rem(i, 4)
         r = first * lax.rem(i, nblk) + (1 - first) * (i // 4)
 
+        @pl.when((first == 1) & (i == 0))
+        def _():
+            step6()
+
         @pl.when((first == 1) & (i == nblk))
         def _():
-            forward(MLP)
-            near(MLP)
+            step7()
 
         @pl.when((first == 1) & (i == 3 * nblk))
         def _():
-            far(MLP)
+            step8()
 
         rows = pl.ds(pl.multiple_of(r * HALF, HALF), HALF)
 
@@ -379,8 +508,22 @@
         drow = dtab[i, dp, pl.ds(row, 1), :]
         out_d[i : i + 1, :] = jnp.where(side == 0, drow, pltpu.roll(drow, 64, 1))[:, :64].astype(BF)
 
-    for copy in [*hop1.values(), *hop2.values(), *d2d.values()]:
-        copy.wait_send()
+    for table in (hop1, hop2, yhop1, yhop2, d2d):
+        for key, copy in table.items():
+            if key[0] != "qkv":
+                copy.wait_send()
+
+    @pl.when(first == 0)
+    def _():
+        for table in (hop1, hop2, d2d):
+            for key, copy in table.items():
+                if key[0] == "qkv":
+                    copy.wait_send()
+
+    @pl.when(first == 1)
+    def _():
+        for k in range(1, 4):
+            share(k).wait_send()
 
     @pl.when(pipe < 3)
     def _():
@@ -420,7 +563,7 @@
             pltpu.VMEM((4, G, D), BF),
             pltpu.VMEM((4, D, D), BF),
             pltpu.VMEM((4, D, D), BF),
-            pltpu.VMEM((S, D), BF),
+            pltpu.VMEM((4, S, D), BF),
             pltpu.VMEM((S, D), BF),
             pltpu.VMEM((3, S, G), BF),
             pltpu.VMEM((4, S, G), BF),
@@ -428,7 +571,7 @@
             pltpu.VMEM((G, S), BF),
             pltpu.VMEM((4, S, G), BF),
             pltpu.VMEM((S, G), F32),
-            pltpu.VMEM((S, D), BF),
+            pltpu.VMEM((8, S, G), BF),
             pltpu.VMEM((S, D), F32),
             pltpu.VMEM((S, D), BF),
             pltpu.VMEM((HALF, D), BF),
@@ -437,7 +580,9 @@
             pltpu.VMEM((16, D), F32),
             pltpu.SemaphoreType.DMA((N_SEMS,)),
             pltpu.SemaphoreType.DMA((N_SEMS,)),
-            pltpu.SemaphoreType.DMA((8,)),
+            pltpu.SemaphoreType.DMA((12,)),
+            pltpu.SemaphoreType.DMA((3,)),
+            pltpu.SemaphoreType.DMA((3,)),
             pltpu.SemaphoreType.DMA((S // HALF,)),
             pltpu.SemaphoreType.DMA((S // HALF,)),
             pltpu.SemaphoreType.DMA((7,)),

time: 296 us -> 272 us (0.919)
  Pallas kernels: 292 us -> 267 us
    pallas_call x1, Pallas kernels: 292 us -> 267 us  [per_device(): pl.pallas_call(kernel, out_shape=(jax.ShapeDtypeStruct((2, 64), BF), jax....]
where the time goes in v2:
time: 272 us; the launch traced here: 271 us
  Pallas kernels  267 us (98%)
  local copies, waits for them, and re-layouts  3.55 us (1%)
    pallas_call x1, Pallas kernels, per_device(): pl.pallas_call(kernel, out_shape=(jax.ShapeDtypeStruct((2, 64), BF), jax....  267 us

profile of v2, /device:TPU:0, one launch (start us, length us, event | category | flops | bytes accessed | tf_op | source)
XLA Modules:
  0.0 271.4 jit_solution(8828810371629184613)
XLA Ops:
  0.6 267.2 %encode.1 = (bf16[2,64]{1,0:T(2,128)(2,1)}, bf16[2,64]{1,0:T(2,128)(2,1)}, f32[2,128]{1,0:T(2,128)}) custom-call(bf16[2,512,1024]{2,1,0:T(8,128)(2,1)} %states_q.1, bf16[2,512,1024]{2,1,0:T(8,128)(2,1)} %states_d.1, s32[2]{0:T(128)} %qlen.1, s32[2]{0:T(128)} %dlen.1, s32[1,2]{1,0:T(1,128)} %order.1, bf16[1,3,1024,256]{3,2,1,0:T(8,128)(2,1)} %w_qkv.1, ...), custom_call_target="tpu_custom_call" | custom-call | tf_op jit(solution)/shard_map/encode/pallas_call | solution.py:556
  267.8 1.3 slice_reduce_fusion
  269.2 1.1 copy.16
  270.3 1.1 copy.17

commit v3 on v2

--- a/solution.py
+++ b/solution.py
@@ -58,8 +58,8 @@
 
 def kernel(
     states_q, states_d, qlen, dlen, order, w_qkv, w_out, w_up, w_down, gain_attn, gain_mlp,
-    out_q, out_d, out_loss,
-    b_qkv, b_out, b_up, b_down, h, hout, qkv, qm, km, kt, vm, cf, ctx, acc, mixed, act, qtab, dtab, tile,
+    out,
+    b_qkv, b_out, b_up, b_down, h, hout, qkv, qm, km, kt, vm, cf, ctx, acc, mixed, act, qtab, dtab, pieces, tile,
     send, recv, local, c_send, c_recv, h_send, h_recv, t1_send, t1_recv, t2_send, t2_recv, t3_send, t3_recv,
 ):
     dp, pipe, z = lax.axis_index("dp"), lax.axis_index("pipe"), lax.axis_index("tensor")
@@ -289,11 +289,6 @@
             device_id=at(pipe_=lax.rem(pipe + 1, 4)), device_id_type=MESH,
         )
 
-    @pl.when(first == 0)
-    def _():
-        for r in range(nblk):
-            hop_x(r).wait_recv()
-
     def length_of(seq):
         return jnp.where(seq == 0, qlen[0], jnp.where(seq == 1, qlen[1], jnp.where(seq == 2, dlen[0], dlen[1])))
 
@@ -304,38 +299,49 @@
     one, zero = jnp.ones((), BF), jnp.zeros((), BF)
 
     @pl.loop(0, 4)
+    def _(k):
+        for r in range(nblk):
+
+            @pl.when((first == 0) & (k == 2 * r))
+            def _():
+                hop_x(r).wait_recv()
+
+        for v in range(2):
+            u = 2 * k + v
+            ahead = first * lax.rem(u // 2 + 1, 4)
+            group = (1 - first) * lax.rem(u, 4)
+            block = first * v + (1 - first) * (u // 4)
+            rows = pl.ds(pl.multiple_of(block * 256, 256), 256)
+            for i in range(3):
+                scale = (0.125 * LOG2E, 1.0, VSCALE)[i]
+                qkv[ahead + group, i, rows, :] = (dot(h[ahead, rows, :], b_qkv[group, i]) * scale).astype(BF)
+
+    @pl.when(first == 1)
+    def _():
+        step1()
+
+    @pl.loop(0, 4)
     def _(j):
         ahead = first * lax.rem(j + 1, 4)
         group = (1 - first) * j
+        at_ = ahead + group
         bias = jnp.where(lax.broadcasted_iota(jnp.int32, (1, S), 1) < length_of(lax.rem(z + ahead, 4)), 0.0, -1e30).astype(BF)
 
-        @pl.when((first == 1) & (j == 1))
-        def _():
-            share(1).start()
-            step1()
-
-        @pl.when((first == 1) & (j == 2))
-        def _():
-            share(2).start()
-            step2()
-
-        @pl.when((first == 1) & (j == 3))
-        def _():
-            share(3).start()
-            step3()
-
-        @pl.loop(0, 3)
-        def _(i):
-            scale = jnp.where(i == 0, 0.125 * LOG2E, jnp.where(i == 2, VSCALE, 1.0)).astype(F32)
-            qkv[i] = (dot(h[ahead], b_qkv[group, i]) * scale).astype(BF)
-
-        kt[...] = qkv[1].T
+        for k in range(1, 4):
+
+            @pl.when((first == 1) & (j == k))
+            def _():
+                share(k).start()
+                if k == 2:
+                    step2()
+
+        kt[...] = qkv[at_, 1].T
         for hd in range(4):
             nxt = (hd + 1) % 4
             mine, other, mark = head == hd, head == nxt, lane == nxt * 64
-            qm[hd] = jnp.where(mine, qkv[0], jnp.where(mark, one, zero))
+            qm[hd] = jnp.where(mine, qkv[at_, 0], jnp.where(mark, one, zero))
             km[hd] = jnp.where(krow == nxt * 64, bias, kt[...])
-            vm[hd] = jnp.where(mine, qkv[2], jnp.where(other, one, zero))
+            vm[hd] = jnp.where(mine, qkv[at_, 2], jnp.where(other, one, zero))
         for hd in range(4):
             mine = head == hd
             for r in range(2):
@@ -350,14 +356,14 @@
 
     @pl.when(first == 1)
     def _():
+        step3()
         step4()
         step5()
         for k in range(1, 4):
             share(k).wait_recv()
 
-    @pl.loop(0, 4)
-    def _(n):
-        cs = pl.ds(pl.multiple_of(n * 256, 256), 256)
+    for n in range(4):
+        cs = slice(n * 256, (n + 1) * 256)
         acc[:, cs] = sum(dot(ctx[j], b_out[j, :, cs]) for j in range(4))
 
     @pl.loop(0, 4)
@@ -385,14 +391,12 @@
 
         rows = pl.ds(pl.multiple_of(r * HALF, HALF), HALF)
 
-        @pl.loop(0, 4)
-        def _(n):
-            cs = pl.ds(pl.multiple_of(n * 256, 256), 256)
+        for n in range(4):
+            cs = slice(n * 256, (n + 1) * 256)
             act[:, cs] = gelu(dot(mixed[rows, :], b_up[j, :, cs])).astype(BF)
 
-        @pl.loop(0, 4)
-        def _(n):
-            cs = pl.ds(pl.multiple_of(n * 256, 256), 256)
+        for n in range(4):
+            cs = slice(n * 256, (n + 1) * 256)
             part = dot(act[...], b_down[j, :, cs])
             acc[rows, cs] = jnp.where(j == 0, part, acc[rows, cs] + part)
 
@@ -429,15 +433,14 @@
             device_id=at(z_=lax.rem(z + k, 4)), device_id_type=MESH,
         )
 
-    def t3(tab, i, k):
-        return pltpu.make_async_remote_copy(
-            src_ref=tab, dst_ref=tab, send_sem=t3_send.at[i, k], recv_sem=t3_recv.at[i], device_id=at(pipe_=k), device_id_type=MESH
+    def t3(k):
+        return pltpu.make_async_remote_copy(
+            src_ref=pieces.at[k], dst_ref=pieces.at[4], send_sem=t3_send.at[k], recv_sem=t3_recv.at[0], device_id=at(pipe_=k), device_id_type=MESH
         )
 
     @pl.when(pipe < 3)
     def _():
-        t3(qtab, 0, 0).wait_recv()
-        t3(dtab, 1, 0).wait_recv()
+        t3(0).wait_recv()
 
     @pl.when(pipe == 3)
     def _():
@@ -486,27 +489,29 @@
             def _():
                 t2(dtab, lax.rem(there, 2), k).wait_recv()
 
-        for k in range(3):
-            t3(qtab, 0, k).start()
-            t3(dtab, 1, k).start()
-
-    doc_dp = lax.broadcasted_iota(jnp.int32, (8, 1), 0)
-    for i in range(2):
-        total, positive = jnp.zeros((1, 1), F32), jnp.zeros((1, 1), F32)
-        for s in range(2):
-            prod = dtab[s] * qtab[i][None]
-            score = jnp.sum(jnp.sum(prod, axis=1), axis=1, keepdims=True) / 0.05
-            total += jnp.sum(jnp.exp(score), axis=0, keepdims=True)
-            hit = (doc_dp == dp) & (order[0, i] == s)
-            positive += jnp.sum(jnp.where(hit, score, 0.0), axis=0, keepdims=True)
-        out_loss[i : i + 1, :] = jnp.broadcast_to(jnp.log(total) - positive, (1, 128))
-    piece = pipe * 4 + z
-    row, side = piece // 2, lax.rem(piece, 2)
-    for i in range(2):
-        qrow = qtab[i, pl.ds(row, 1), :]
-        out_q[i : i + 1, :] = jnp.where(side == 0, qrow, pltpu.roll(qrow, 64, 1))[:, :64].astype(BF)
-        drow = dtab[i, dp, pl.ds(row, 1), :]
-        out_d[i : i + 1, :] = jnp.where(side == 0, drow, pltpu.roll(drow, 64, 1))[:, :64].astype(BF)
+        doc_dp = lax.broadcasted_iota(jnp.int32, (8, 1), 0)
+        losses = []
+        for i in range(2):
+            total, positive = jnp.zeros((1, 1), F32), jnp.zeros((1, 1), F32)
+            for s in range(2):
+                prod = dtab[s] * qtab[i][None]
+                score = jnp.sum(jnp.sum(prod, axis=1), axis=1, keepdims=True) / 0.05
+                total += jnp.sum(jnp.exp(score), axis=0, keepdims=True)
+                hit = (doc_dp == dp) & (order[0, i] == s)
+                positive += jnp.sum(jnp.where(hit, score, 0.0), axis=0, keepdims=True)
+            losses.append(jnp.broadcast_to(jnp.log(total) - positive, (1, 128)))
+        for k in (0, 1, 2, 3):
+            row = 2 * k + z // 2
+            pieces[k, 6:8, :] = jnp.zeros((2, 128), F32)
+            for i in range(2):
+                for at_row, line in ((i, qtab[i, pl.ds(row, 1), :]), (2 + i, dtab[i, dp, pl.ds(row, 1), :])):
+                    pieces[k, at_row : at_row + 1, :] = jnp.where(z_low == 0, line, pltpu.roll(line, 64, 1))
+                pieces[k, 4 + i : 5 + i, :] = losses[i]
+            if k < 3:
+                t3(k).start()
+        pieces[4] = pieces[3]
+
+    out[...] = pieces[4]
 
     for table in (hop1, hop2, yhop1, yhop2, d2d):
         for key, copy in table.items():
@@ -533,8 +538,7 @@
     @pl.when(pipe == 3)
     def _():
         for k in range(3):
-            t3(qtab, 0, k).wait_send()
-            t3(dtab, 1, k).wait_send()
+            t3(k).wait_send()
 
         @pl.when(z >= 2)
         def _():
@@ -553,11 +557,11 @@
     anyspace = pl.BlockSpec(memory_space=pl.ANY)
     smem = pl.BlockSpec(memory_space=pltpu.SMEM)
     vmem = pl.BlockSpec(memory_space=pltpu.VMEM)
-    q, d, loss = pl.pallas_call(
+    out = pl.pallas_call(
         kernel,
-        out_shape=(jax.ShapeDtypeStruct((2, 64), BF), jax.ShapeDtypeStruct((2, 64), BF), jax.ShapeDtypeStruct((2, 128), F32)),
+        out_shape=jax.ShapeDtypeStruct((8, 128), F32),
         in_specs=[anyspace, anyspace, smem, smem, smem, *[anyspace] * 6],
-        out_specs=(vmem, vmem, vmem),
+        out_specs=vmem,
         scratch_shapes=[
             pltpu.VMEM((4, 3, D, G), BF),
             pltpu.VMEM((4, G, D), BF),
@@ -565,7 +569,7 @@
             pltpu.VMEM((4, D, D), BF),
             pltpu.VMEM((4, S, D), BF),
             pltpu.VMEM((S, D), BF),
-            pltpu.VMEM((3, S, G), BF),
+            pltpu.VMEM((4, 3, S, G), BF),
             pltpu.VMEM((4, S, G), BF),
             pltpu.VMEM((4, G, S), BF),
             pltpu.VMEM((G, S), BF),
@@ -577,6 +581,7 @@
             pltpu.VMEM((HALF, D), BF),
             pltpu.VMEM((2, 8, 128), F32),
             pltpu.VMEM((2, 8, 8, 128), F32),
+            pltpu.VMEM((5, 8, 128), F32),
             pltpu.VMEM((16, D), F32),
             pltpu.SemaphoreType.DMA((N_SEMS,)),
             pltpu.SemaphoreType.DMA((N_SEMS,)),
@@ -589,13 +594,13 @@
             pltpu.SemaphoreType.DMA((7,)),
             pltpu.SemaphoreType.DMA((3,)),
             pltpu.SemaphoreType.DMA((3,)),
-            pltpu.SemaphoreType.DMA((2, 3)),
-            pltpu.SemaphoreType.DMA((2,)),
+            pltpu.SemaphoreType.DMA((3,)),
+            pltpu.SemaphoreType.DMA((1,)),
         ],
         compiler_params=pltpu.CompilerParams(collective_id=0, has_side_effects=True, vmem_limit_bytes=63 * 2**20),
         name="encode",
     )(query_states, doc_states, query_len, doc_len, doc_order, w_qkv, w_out, w_up, w_down, gain_attn, gain_mlp)
-    return q, d, loss[:, 0]
+    return out[0:2, :64].astype(BF), out[2:4, :64].astype(BF), out[4:6, 0]
 
 
 def solution(mesh):

time: 272 us -> 227 us (0.83)
  Pallas kernels: 267 us -> 224 us
    pallas_call x1, Pallas kernels: 267 us -> 224 us  [per_device(): pl.pallas_call(kernel, out_shape=jax.ShapeDtypeStruct((8, 128), F32), in_...]
where the time goes in v3:
time: 227 us
  Pallas kernels  224 us (99%)
    pallas_call x1, Pallas kernels, per_device(): pl.pallas_call(kernel, out_shape=jax.ShapeDtypeStruct((8, 128), F32), in_...  224 us

profile of v3, /device:TPU:0, one launch (start us, length us, event | category | flops | bytes accessed | tf_op | source)
XLA Modules:
  0.0 227.3 jit_solution(3567769152988823678)
XLA Ops:
  0.6 224.2 %encode.1 = f32[8,128]{1,0:T(8,128)} custom-call(bf16[2,512,1024]{2,1,0:T(8,128)(2,1)} %states_q.1, bf16[2,512,1024]{2,1,0:T(8,128)(2,1)} %states_d.1, s32[2]{0:T(128)} %qlen.1, s32[2]{0:T(128)} %dlen.1, s32[1,2]{1,0:T(1,128)} %order.1, bf16[1,3,1024,256]{3,2,1,0:T(8,128)(2,1)} %w_qkv.1, bf16[1,256,1024]{2,1,0:T(8,128)(2,1)} %w_out.1, ...), custom_call_target="tpu_custom_call" | custom-call | tf_op jit(solution)/shard_map/encode/pallas_call | solution.py:560
  224.8 1.3 slice_reduce_fusion
  226.1 0.7 convert.4
  226.8 0.5 fusion

commit v4 on v3

--- a/solution.py
+++ b/solution.py
@@ -59,7 +59,7 @@
 def kernel(
     states_q, states_d, qlen, dlen, order, w_qkv, w_out, w_up, w_down, gain_attn, gain_mlp,
     out,
-    b_qkv, b_out, b_up, b_down, h, hout, qkv, qm, km, kt, vm, cf, ctx, acc, mixed, act, qtab, dtab, pieces, tile,
+    b_qkv, b_out, b_up, b_down, h, hout, qkv, qm, km, kt, vm, cf, ctx, relay, acc, mixed, act, qtab, dtab, pieces, tile,
     send, recv, local, c_send, c_recv, h_send, h_recv, t1_send, t1_recv, t2_send, t2_recv, t3_send, t3_recv,
 ):
     dp, pipe, z = lax.axis_index("dp"), lax.axis_index("pipe"), lax.axis_index("tensor")
@@ -170,45 +170,45 @@
             d2d[name, slot].start()
 
     def begin_all():
+        begin("out", "Z")
         begin("up", "Q")
         begin("down", "Q")
 
     def step1():
+        z_near("out", "Z")
+        give("out", 1, 2)
+
+    def step2():
         z_near("up", "Q")
         y_begin("up", 1, 2)
 
-    def step2():
-        begin("out", "Z")
+    def step3():
         z_near("down", "Q")
         y_begin("down", 1, 2)
 
-    def step3():
+    def step4():
+        z_far("out", "Z")
+        give("out", 3)
+        z_far("up", "Q")
+        y_begin("up", 3)
+        y_on("up", 1, 2)
+
+    def step5():
         begin("up", "Z")
         begin("down", "Z")
-        z_far("up", "Q")
-        y_begin("up", 3)
-
-    def step4():
+        y_on("down", 1, 2)
         z_far("down", "Q")
         y_begin("down", 3)
-        z_near("out", "Z")
-        give("out", 1, 2)
-        y_on("up", 1, 2)
-
-    def step5():
+        arrive("out", 1, 2, 3)
+
+    def step6():
+        y_on("up", 3)
+
+    def step7():
         z_near("up", "Z")
-        z_far("out", "Z")
-        give("out", 3)
-        arrive("out", 1, 2, 3)
-
-    def step6():
-        y_on("down", 1, 2)
-        z_near("down", "Z")
-
-    def step7():
-        y_on("up", 3)
         y_end("up", 1, 2)
         y_on("down", 3)
+        z_near("down", "Z")
         y_end("down", 1, 2)
         arrive("up", 1, 2)
         arrive("down", 1, 2)
@@ -250,17 +250,17 @@
     @pl.when(first == 0)
     def _():
         step1()
+        step2()
         begin("qkv", "Z")
-        step2()
         step3()
+        step4()
+        step5()
         z_near("qkv", "Z")
         give("qkv", 1, 2)
-        step4()
-        step5()
         step6()
+        step7()
         z_far("qkv", "Z")
         give("qkv", 3)
-        step7()
         step8()
         arrive("qkv", 1, 2, 3)
 
@@ -274,11 +274,18 @@
         for k in range(4):
             input_copy(states_q, 0, k).wait()
 
-    def share(k):
-        return pltpu.make_async_remote_copy(
-            src_ref=ctx.at[4 + k], dst_ref=ctx.at[(0, 1, 3, 2)[k]], send_sem=c_send.at[k - 1], recv_sem=c_recv.at[k - 1],
-            device_id=at(z_=lax.rem(z + k, 4)), device_id_type=MESH,
-        )
+    def to_z(i, src, dst, k):
+        return pltpu.make_async_remote_copy(
+            src_ref=src, dst_ref=dst, send_sem=c_send.at[i], recv_sem=c_recv.at[i], device_id=at(z_=lax.rem(z + k, 4)), device_id_type=MESH
+        )
+
+    top, bottom = pl.ds(0, 256), pl.ds(256, 256)
+    share = {
+        1: (to_z(0, ctx.at[5], ctx.at[1], 1),),
+        3: (to_z(1, ctx.at[7], ctx.at[2], 3),),
+        2: (to_z(2, ctx.at[6, top], relay.at[0], 1), to_z(3, ctx.at[6, bottom], relay.at[1], 3)),
+    }
+    share_on = (to_z(4, relay.at[0], ctx.at[3, top], 1), to_z(5, relay.at[1], ctx.at[3, bottom], 3))
 
     nblk = S // HALF
 
@@ -305,6 +312,10 @@
             @pl.when((first == 0) & (k == 2 * r))
             def _():
                 hop_x(r).wait_recv()
+
+        @pl.when((first == 1) & (k == 3))
+        def _():
+            step1()
 
         for v in range(2):
             u = 2 * k + v
@@ -316,103 +327,124 @@
                 scale = (0.125 * LOG2E, 1.0, VSCALE)[i]
                 qkv[ahead + group, i, rows, :] = (dot(h[ahead, rows, :], b_qkv[group, i]) * scale).astype(BF)
 
-    @pl.when(first == 1)
-    def _():
-        step1()
-
     @pl.loop(0, 4)
-    def _(j):
-        ahead = first * lax.rem(j + 1, 4)
-        group = (1 - first) * j
-        at_ = ahead + group
-        bias = jnp.where(lax.broadcasted_iota(jnp.int32, (1, S), 1) < length_of(lax.rem(z + ahead, 4)), 0.0, -1e30).astype(BF)
-
-        for k in range(1, 4):
-
-            @pl.when((first == 1) & (j == k))
-            def _():
-                share(k).start()
-                if k == 2:
-                    step2()
-
-        kt[...] = qkv[at_, 1].T
-        for hd in range(4):
-            nxt = (hd + 1) % 4
-            mine, other, mark = head == hd, head == nxt, lane == nxt * 64
-            qm[hd] = jnp.where(mine, qkv[at_, 0], jnp.where(mark, one, zero))
-            km[hd] = jnp.where(krow == nxt * 64, bias, kt[...])
-            vm[hd] = jnp.where(mine, qkv[at_, 2], jnp.where(other, one, zero))
-        for hd in range(4):
-            mine = head == hd
-            for r in range(2):
-                rows = slice(r * 256, (r + 1) * 256)
-                p = jnp.exp2(dot(qm[hd, rows, :], km[hd])).astype(BF)
-                o = dot(p, vm[hd])
-                total = pltpu.roll(o, 192, 1)
-                t = jnp.where(total > 2.0**60, 2.0**-64, 1.0).astype(F32)
-                c = (o * t) * (1.0 / (total * t)) * (1.0 / VSCALE)
-                cf[rows, :] = jnp.where(mine, c, cf[rows, :] if hd else c)
-        ctx[group + ahead + 4 * ((ahead + 3) // 4)] = cf[...].astype(BF)
-
-    @pl.when(first == 1)
-    def _():
-        step3()
-        step4()
-        step5()
-        for k in range(1, 4):
-            share(k).wait_recv()
-
-    for n in range(4):
-        cs = slice(n * 256, (n + 1) * 256)
-        acc[:, cs] = sum(dot(ctx[j], b_out[j, :, cs]) for j in range(4))
-
-    @pl.loop(0, 4)
-    def _(r):
-        for q in range(4):
-            rows = pl.ds(pl.multiple_of(r * 128 + q * 32, 32), 32)
-            mixed[rows, :] = norm_rows(h[0, rows, :].astype(F32) + acc[rows, :], tile[0:1, :]).astype(BF)
-
-    @pl.loop(0, 4 * nblk)
-    def _(i):
-        j = first * (i // nblk) + (1 - first) * lax.rem(i, 4)
-        r = first * lax.rem(i, nblk) + (1 - first) * (i // 4)
-
-        @pl.when((first == 1) & (i == 0))
+    def _(g):
+        kt[g] = qkv[g, 1].T
+
+    def order_of(t):
+        return lax.rem(2 + 3 * t + 3 * (t // 2) + 2 * (t // 3), 4)
+
+    @pl.loop(0, 2 - first)
+    def _(blk):
+        @pl.loop(0, 2 + 2 * first)
+        def _(t):
+            @pl.when((first == 1) & (t == 1))
+            def _():
+                step2()
+                for copy in share[2]:
+                    copy.start()
+
+            @pl.when((first == 1) & (t == 2))
+            def _():
+                for copy in share[1]:
+                    copy.start()
+
+            @pl.when((first == 1) & (t == 3))
+            def _():
+                for copy in share[3]:
+                    copy.start()
+                step3()
+
+            ahead = order_of(t)
+            for v in range(2):
+                group = first * ahead + (1 - first) * (2 * t + v)
+                block = first * v + (1 - first) * blk
+                rows = pl.ds(pl.multiple_of(block * 256, 256), 256)
+                for hd in range(4):
+                    nxt = (hd + 1) % 4
+                    mine, other, mark = head == hd, head == nxt, lane == nxt * 64
+                    seq = lax.rem(z + first * ahead, 4)
+                    bias = jnp.where(lax.broadcasted_iota(jnp.int32, (1, S), 1) < length_of(seq), 0.0, -1e30).astype(BF)
+                    qm[v, hd] = jnp.where(mine, qkv[group, 0, rows, :], jnp.where(mark, one, zero))
+                    km[v, hd] = jnp.where(krow == nxt * 64, bias, kt[group])
+                    vm[v, hd] = jnp.where(mine, qkv[group, 2], jnp.where(other, one, zero))
+            for hd in range(4):
+                mine = head == hd
+                for v in range(2):
+                    p = jnp.exp2(dot(qm[v, hd], km[v, hd])).astype(BF)
+                    o = dot(p, vm[v, hd])
+                    total = pltpu.roll(o, 192, 1)
+                    scale = jnp.where(total > 2.0**60, 2.0**-64, 1.0).astype(F32)
+                    c = (o * scale) * (1.0 / (total * scale)) * (1.0 / VSCALE)
+                    cf[v] = jnp.where(mine, c, cf[v] if hd else c)
+            for v in range(2):
+                group = first * (ahead + 4 * ((ahead + 3) // 4)) + (1 - first) * (2 * t + v)
+                block = first * v + (1 - first) * blk
+                ctx[group, pl.ds(pl.multiple_of(block * 256, 256), 256), :] = cf[v].astype(BF)
+
+        @pl.when(first == 1)
         def _():
-            step6()
-
-        @pl.when((first == 1) & (i == nblk))
-        def _():
-            step7()
-
-        @pl.when((first == 1) & (i == 3 * nblk))
-        def _():
-            step8()
-
-        rows = pl.ds(pl.multiple_of(r * HALF, HALF), HALF)
-
-        for n in range(4):
-            cs = slice(n * 256, (n + 1) * 256)
-            act[:, cs] = gelu(dot(mixed[rows, :], b_up[j, :, cs])).astype(BF)
-
-        for n in range(4):
-            cs = slice(n * 256, (n + 1) * 256)
-            part = dot(act[...], b_down[j, :, cs])
-            acc[rows, cs] = jnp.where(j == 0, part, acc[rows, cs] + part)
-
-        @pl.when(j == 3)
-        def _():
-            @pl.loop(0, HALF // 64)
+            step4()
+            for here, on in zip(share[2], share_on):
+                here.wait_recv()
+                on.start()
+            step5()
+            for copy in (*share[1], *share[3], *share_on):
+                copy.wait_recv()
+
+        @pl.loop(0, 1 + first)
+        def _(b):
+            base = (blk + b) * 256
+            rows = pl.ds(pl.multiple_of(base, 256), 256)
+            for n in range(4):
+                cs = slice(n * 256, (n + 1) * 256)
+                acc[rows, cs] = sum(dot(ctx[j, rows, :], b_out[j, :, cs]) for j in range(4))
+
+            @pl.loop(0, 4)
             def _(q):
                 for u in range(2):
-                    rr = pl.ds(pl.multiple_of(r * HALF + q * 64 + u * 32, 32), 32)
-                    hout[rr, :] = norm_rows(mixed[rr, :].astype(F32) + acc[rr, :], tile[8:9, :]).astype(BF)
-
-            for rs in range(nblk):
-
-                @pl.when((pipe < 3) & (r == rs))
-                def _():
-                    hop_x(rs).start()
+                    rr = pl.ds(pl.multiple_of(base + q * 64 + u * 32, 32), 32)
+                    mixed[rr, :] = norm_rows(h[0, rr, :].astype(F32) + acc[rr, :], tile[0:1, :]).astype(BF)
+
+        @pl.loop(0, 4 + 4 * first)
+        def _(i):
+            j = first * (i // 2) + (1 - first) * i
+            r = first * lax.rem(i, 2) + (1 - first) * blk
+
+            @pl.when((first == 1) & (i == 0))
+            def _():
+                step6()
+
+            @pl.when((first == 1) & (i == 2))
+            def _():
+                step7()
+
+            @pl.when((first == 1) & (i == 6))
+            def _():
+                step8()
+
+            rows = pl.ds(pl.multiple_of(r * HALF, HALF), HALF)
+            for n in range(4):
+                cs = slice(n * 256, (n + 1) * 256)
+                act[:, cs] = gelu(dot(mixed[rows, :], b_up[j, :, cs])).astype(BF)
+            for n in range(4):
+                cs = slice(n * 256, (n + 1) * 256)
+                part = dot(act[...], b_down[j, :, cs])
+                acc[rows, cs] = jnp.where(j == 0, part, acc[rows, cs] + part)
+
+            @pl.when(j == 3)
+            def _():
+                @pl.loop(0, 4)
+                def _(q):
+                    for u in range(2):
+                        rr = pl.ds(pl.multiple_of(r * HALF + q * 64 + u * 32, 32), 32)
+                        hout[rr, :] = norm_rows(mixed[rr, :].astype(F32) + acc[rr, :], tile[8:9, :]).astype(BF)
+
+                for rs in range(nblk):
+
+                    @pl.when((pipe < 3) & (r == rs))
+                    def _():
+                        hop_x(rs).start()
 
     def t1(k):
         return pltpu.make_async_remote_copy(
@@ -527,8 +559,8 @@
 
     @pl.when(first == 1)
     def _():
-        for k in range(1, 4):
-            share(k).wait_send()
+        for copy in (*share[1], *share[2], *share[3], *share_on):
+            copy.wait_send()
 
     @pl.when(pipe < 3)
     def _():
@@ -570,12 +602,13 @@
             pltpu.VMEM((4, S, D), BF),
             pltpu.VMEM((S, D), BF),
             pltpu.VMEM((4, 3, S, G), BF),
-            pltpu.VMEM((4, S, G), BF),
+            pltpu.VMEM((2, 4, 256, G), BF),
+            pltpu.VMEM((2, 4, G, S), BF),
             pltpu.VMEM((4, G, S), BF),
-            pltpu.VMEM((G, S), BF),
-            pltpu.VMEM((4, S, G), BF),
-            pltpu.VMEM((S, G), F32),
+            pltpu.VMEM((2, 4, S, G), BF),
+            pltpu.VMEM((2, 256, G), F32),
             pltpu.VMEM((8, S, G), BF),
+            pltpu.VMEM((2, 256, G), BF),
             pltpu.VMEM((S, D), F32),
             pltpu.VMEM((S, D), BF),
             pltpu.VMEM((HALF, D), BF),
@@ -586,8 +619,8 @@
             pltpu.SemaphoreType.DMA((N_SEMS,)),
             pltpu.SemaphoreType.DMA((N_SEMS,)),
             pltpu.SemaphoreType.DMA((12,)),
-            pltpu.SemaphoreType.DMA((3,)),
-            pltpu.SemaphoreType.DMA((3,)),
+            pltpu.SemaphoreType.DMA((6,)),
+            pltpu.SemaphoreType.DMA((6,)),
             pltpu.SemaphoreType.DMA((S // HALF,)),
             pltpu.SemaphoreType.DMA((S // HALF,)),
             pltpu.SemaphoreType.DMA((7,)),

time: 227 us -> 204 us (0.90)
  Pallas kernels: 224 us -> 200 us
    pallas_call x1, Pallas kernels: 224 us -> 200 us  [per_device(): pl.pallas_call(kernel, out_shape=jax.ShapeDtypeStruct((8, 128), F32), in_...]
where the time goes in v4:
time: 204 us
  Pallas kernels  200 us (98%)
    pallas_call x1, Pallas kernels, per_device(): pl.pallas_call(kernel, out_shape=jax.ShapeDtypeStruct((8, 128), F32), in_...  200 us

profile of v4, /device:TPU:0, one launch (start us, length us, event | category | flops | bytes accessed | tf_op | source)
XLA Modules:
  0.0 203.6 jit_solution(12442063801554022744)
XLA Ops:
  0.6 200.4 %encode.1 = f32[8,128]{1,0:T(8,128)} custom-call(bf16[2,512,1024]{2,1,0:T(8,128)(2,1)} %states_q.1, bf16[2,512,1024]{2,1,0:T(8,128)(2,1)} %states_d.1, s32[2]{0:T(128)} %qlen.1, s32[2]{0:T(128)} %dlen.1, s32[1,2]{1,0:T(1,128)} %order.1, bf16[1,3,1024,256]{3,2,1,0:T(8,128)(2,1)} %w_qkv.1, bf16[1,256,1024]{2,1,0:T(8,128)(2,1)} %w_out.1, ...), custom_call_target="tpu_custom_call" | custom-call | tf_op jit(solution)/shard_map/encode/pallas_call | solution.py:592
  201.1 1.3 slice_reduce_fusion
  202.4 0.7 convert.4
  203.1 0.5 fusion

commit v5 on v4

--- a/solution.py
+++ b/solution.py
@@ -9,6 +9,8 @@
 D = 1024
 G = 256
 HALF = 256
+DIRECT = 176
+CHUNKS = ((176, 48), (224, 32))
 BF = jnp.bfloat16
 F32 = jnp.float32
 LOG2E = 1.4426950408889634
@@ -59,8 +61,8 @@
 def kernel(
     states_q, states_d, qlen, dlen, order, w_qkv, w_out, w_up, w_down, gain_attn, gain_mlp,
     out,
-    b_qkv, b_out, b_up, b_down, h, hout, qkv, qm, km, kt, vm, cf, ctx, relay, acc, mixed, act, qtab, dtab, pieces, tile,
-    send, recv, local, c_send, c_recv, h_send, h_recv, t1_send, t1_recv, t2_send, t2_recv, t3_send, t3_recv,
+    b_qkv, b_out, b_up, b_down, h, hout, qkv, qm, km, kt, vm, cf, tf, ctx, relay, hrelay, acc, mixed, act, qtab, dtab, pieces, tile,
+    send, recv, local, c_send, c_recv, h_send, h_recv, w_send, w_recv, t1_send, t1_recv, t2_send, t2_recv, t3_send, t3_recv,
 ):
     dp, pipe, z = lax.axis_index("dp"), lax.axis_index("pipe"), lax.axis_index("tensor")
     core = lax.rem(dp, 2)
@@ -221,8 +223,7 @@
         arrive("up", 3)
         arrive("down", 3)
 
-    for name in ARRAYS:
-        loads[name].start()
+    loads["qkv"].start()
     gains = [pltpu.make_async_copy(gain_attn, tile.at[pl.ds(0, 1)], local.at[4]), pltpu.make_async_copy(gain_mlp, tile.at[pl.ds(8, 1)], local.at[5])]
     for g in gains:
         g.start()
@@ -243,8 +244,88 @@
             def _():
                 input_copy(states_d, lax.rem(seq, 2), k).start()
 
+    for name in ("out", *MLP):
+        loads[name].start()
     pl.semaphore_wait(barrier, 13)
     begin_all()
+    nblk = S // HALF
+
+    def hop_x(r, size=HALF):
+        rows = pl.ds(r * HALF, size)
+        return pltpu.make_async_remote_copy(
+            src_ref=hout.at[rows], dst_ref=h.at[0, rows], send_sem=h_send.at[r], recv_sem=h_recv.at[r],
+            device_id=at(pipe_=lax.rem(pipe + 1, 4)), device_id_type=MESH,
+        )
+
+    chunks = [(r, c) for r in range(nblk) for c in range(len(CHUNKS))]
+
+    def way_round(r, c, src, dst):
+        start, size = CHUNKS[c]
+        here, there = pl.ds(r * HALF + start, size), pl.ds(r * (HALF - DIRECT) + start - DIRECT, size)
+        pick = {"out": hout.at[here], "relay": hrelay.at[there], "in": h.at[0, here]}
+        return pltpu.make_async_remote_copy(
+            src_ref=pick[src], dst_ref=pick[dst], send_sem=w_send.at[r * len(CHUNKS) + c], recv_sem=w_recv.at[r * len(CHUNKS) + c],
+            device_id=at(pipe_=lax.rem(pipe + 3, 4)), device_id_type=MESH,
+        )
+
+    def send_on(r):
+        @pl.when(first == 1)
+        def _():
+            for c in range(len(CHUNKS)):
+                way_round(r, c, "out", "relay").start()
+            hop_x(r, DIRECT).start()
+
+        @pl.when((pipe == 1) | (pipe == 2))
+        def _():
+            hop_x(r).start()
+
+    def take(r):
+        @pl.when(pipe == 1)
+        def _():
+            hop_x(r, DIRECT).wait_recv()
+            for c in range(len(CHUNKS)):
+                way_round(r, c, "relay", "in").wait_recv()
+
+        @pl.when(pipe >= 2)
+        def _():
+            hop_x(r).wait_recv()
+
+    def pass_on():
+        @pl.when(pipe == 3)
+        def _():
+            for r, c in chunks:
+                way_round(r, c, "out", "relay").wait_recv()
+                way_round(r, c, "relay", "relay").start()
+
+        @pl.when(pipe == 2)
+        def _():
+            for r, c in chunks:
+                way_round(r, c, "relay", "relay").wait_recv()
+                way_round(r, c, "relay", "in").start()
+
+    def sent():
+        @pl.when(first == 1)
+        def _():
+            for r, c in chunks:
+                way_round(r, c, "out", "relay").wait_send()
+            for r in range(nblk):
+                hop_x(r, DIRECT).wait_send()
+
+        @pl.when((pipe == 1) | (pipe == 2))
+        def _():
+            for r in range(nblk):
+                hop_x(r).wait_send()
+
+        @pl.when(pipe == 3)
+        def _():
+            for r, c in chunks:
+                way_round(r, c, "relay", "relay").wait_send()
+
+        @pl.when(pipe == 2)
+        def _():
+            for r, c in chunks:
+                way_round(r, c, "relay", "in").wait_send()
+
     z_low = lax.rem(z, 2)
 
     @pl.when(first == 0)
@@ -259,15 +340,13 @@
         give("qkv", 1, 2)
         step6()
         step7()
+        pass_on()
         z_far("qkv", "Z")
         give("qkv", 3)
         step8()
         arrive("qkv", 1, 2, 3)
 
-    for name in ARRAYS:
-        loads[name].wait()
-    for g in gains:
-        g.wait()
+    loads["qkv"].wait()
 
     @pl.when(first == 1)
     def _():
@@ -287,15 +366,6 @@
     }
     share_on = (to_z(4, relay.at[0], ctx.at[3, top], 1), to_z(5, relay.at[1], ctx.at[3, bottom], 3))
 
-    nblk = S // HALF
-
-    def hop_x(r):
-        rows = pl.ds(r * HALF, HALF)
-        return pltpu.make_async_remote_copy(
-            src_ref=hout.at[rows], dst_ref=h.at[0, rows], send_sem=h_send.at[r], recv_sem=h_recv.at[r],
-            device_id=at(pipe_=lax.rem(pipe + 1, 4)), device_id_type=MESH,
-        )
-
     def length_of(seq):
         return jnp.where(seq == 0, qlen[0], jnp.where(seq == 1, qlen[1], jnp.where(seq == 2, dlen[0], dlen[1])))
 
@@ -311,7 +381,7 @@
 
             @pl.when((first == 0) & (k == 2 * r))
             def _():
-                hop_x(r).wait_recv()
+                take(r)
 
         @pl.when((first == 1) & (k == 3))
         def _():
@@ -330,6 +400,11 @@
     @pl.loop(0, 4)
     def _(g):
         kt[g] = qkv[g, 1].T
+
+    for name in ("out", *MLP):
+        loads[name].wait()
+    for g in gains:
+        g.wait()
 
     def order_of(t):
         return lax.rem(2 + 3 * t + 3 * (t // 2) + 2 * (t // 3), 4)
@@ -373,14 +448,15 @@
                 for v in range(2):
                     p = jnp.exp2(dot(qm[v, hd], km[v, hd])).astype(BF)
                     o = dot(p, vm[v, hd])
-                    total = pltpu.roll(o, 192, 1)
-                    scale = jnp.where(total > 2.0**60, 2.0**-64, 1.0).astype(F32)
-                    c = (o * scale) * (1.0 / (total * scale)) * (1.0 / VSCALE)
-                    cf[v] = jnp.where(mine, c, cf[v] if hd else c)
+                    cf[v] = jnp.where(mine, o, cf[v]) if hd else o
+                    tf[v] = jnp.where(head == (hd + 1) % 4, o, tf[v]) if hd else o
             for v in range(2):
+                total = pltpu.roll(tf[v], 192, 1)
+                scale = jnp.where(total > 2.0**60, 2.0**-64, 1.0).astype(F32)
+                c = (cf[v] * scale) * (1.0 / (total * scale)) * (1.0 / VSCALE)
                 group = first * (ahead + 4 * ((ahead + 3) // 4)) + (1 - first) * (2 * t + v)
                 block = first * v + (1 - first) * blk
-                ctx[group, pl.ds(pl.multiple_of(block * 256, 256), 256), :] = cf[v].astype(BF)
+                ctx[group, pl.ds(pl.multiple_of(block * 256, 256), 256), :] = c.astype(BF)
 
         @pl.when(first == 1)
         def _():
@@ -400,10 +476,10 @@
                 cs = slice(n * 256, (n + 1) * 256)
                 acc[rows, cs] = sum(dot(ctx[j, rows, :], b_out[j, :, cs]) for j in range(4))
 
-            @pl.loop(0, 4)
+            @pl.loop(0, 2)
             def _(q):
-                for u in range(2):
-                    rr = pl.ds(pl.multiple_of(base + q * 64 + u * 32, 32), 32)
+                for u in range(4):
+                    rr = pl.ds(pl.multiple_of(base + q * 128 + u * 32, 32), 32)
                     mixed[rr, :] = norm_rows(h[0, rr, :].astype(F32) + acc[rr, :], tile[0:1, :]).astype(BF)
 
         @pl.loop(0, 4 + 4 * first)
@@ -434,17 +510,17 @@
 
             @pl.when(j == 3)
             def _():
-                @pl.loop(0, 4)
+                @pl.loop(0, 2)
                 def _(q):
-                    for u in range(2):
-                        rr = pl.ds(pl.multiple_of(r * HALF + q * 64 + u * 32, 32), 32)
+                    for u in range(4):
+                        rr = pl.ds(pl.multiple_of(r * HALF + q * 128 + u * 32, 32), 32)
                         hout[rr, :] = norm_rows(mixed[rr, :].astype(F32) + acc[rr, :], tile[8:9, :]).astype(BF)
 
                 for rs in range(nblk):
 
                     @pl.when((pipe < 3) & (r == rs))
                     def _():
-                        hop_x(rs).start()
+                        send_on(rs)
 
     def t1(k):
         return pltpu.make_async_remote_copy(
@@ -562,10 +638,7 @@
         for copy in (*share[1], *share[2], *share[3], *share_on):
             copy.wait_send()
 
-    @pl.when(pipe < 3)
-    def _():
-        for r in range(nblk):
-            hop_x(r).wait_send()
+    sent()
 
     @pl.when(pipe == 3)
     def _():
@@ -583,6 +656,13 @@
         def _():
             for k in range(1, 4):
                 t2(qtab, z_low, k).wait_send()
+
+
+def split(tile, out_q, out_d, out_loss):
+    out_q[...] = tile[0:2, :64].astype(BF)
+    out_d[...] = tile[2:4, :64].astype(BF)
+    for i in range(2):
+        out_loss[i] = tile[4 + i, 0]
 
 
 def per_device(query_states, doc_states, query_len, doc_len, doc_order, w_qkv, w_out, w_up, w_down, gain_attn, gain_mlp):
@@ -607,8 +687,10 @@
             pltpu.VMEM((4, G, S), BF),
             pltpu.VMEM((2, 4, S, G), BF),
             pltpu.VMEM((2, 256, G), F32),
+            pltpu.VMEM((2, 256, G), F32),
             pltpu.VMEM((8, S, G), BF),
             pltpu.VMEM((2, 256, G), BF),
+            pltpu.VMEM((2 * (HALF - DIRECT), D), BF),
             pltpu.VMEM((S, D), F32),
             pltpu.VMEM((S, D), BF),
             pltpu.VMEM((HALF, D), BF),
@@ -623,6 +705,8 @@
             pltpu.SemaphoreType.DMA((6,)),
             pltpu.SemaphoreType.DMA((S // HALF,)),
             pltpu.SemaphoreType.DMA((S // HALF,)),
+            pltpu.SemaphoreType.DMA((4,)),
+            pltpu.SemaphoreType.DMA((4,)),
             pltpu.SemaphoreType.DMA((7,)),
             pltpu.SemaphoreType.DMA((7,)),
             pltpu.SemaphoreType.DMA((3,)),
@@ -633,7 +717,13 @@
         compiler_params=pltpu.CompilerParams(collective_id=0, has_side_effects=True, vmem_limit_bytes=63 * 2**20),
         name="encode",
     )(query_states, doc_states, query_len, doc_len, doc_order, w_qkv, w_out, w_up, w_down, gain_attn, gain_mlp)
-    return out[0:2, :64].astype(BF), out[2:4, :64].astype(BF), out[4:6, 0]
+    return pl.pallas_call(
+        split,
+        out_shape=(jax.ShapeDtypeStruct((2, 64), BF), jax.ShapeDtypeStruct((2, 64), BF), jax.ShapeDtypeStruct((2,), F32)),
+        in_specs=[vmem],
+        out_specs=(vmem, vmem, smem),
+        name="split",
+    )(out)
 
 
 def solution(mesh):

time: 204 us -> 192 us (0.941)
  Pallas kernels: 200 us -> 191 us
    pallas_call x1, Pallas kernels: 200 us -> 190 us  [per_device(): pl.pallas_call(kernel, out_shape=jax.ShapeDtypeStruct((8, 128), F32), in_...]
where the time goes in v5:
time: 192 us
  Pallas kernels  191 us (99%)
    pallas_call x1, Pallas kernels, per_device(): pl.pallas_call(kernel, out_shape=jax.ShapeDtypeStruct((8, 128), F32), in_...  190 us

profile of v5, /device:TPU:0, one launch (start us, length us, event | category | flops | bytes accessed | tf_op | source)
XLA Modules:
  0.0 191.5 jit_solution(13808884963300256034)
XLA Ops:
  0.6 189.6 %encode.1.tile = f32[8,128]{1,0:T(8,128)} custom-call(bf16[2,512,1024]{2,1,0:T(8,128)(2,1)} %states_q.1, bf16[2,512,1024]{2,1,0:T(8,128)(2,1)} %states_d.1, s32[2]{0:T(128)} %qlen.1, s32[2]{0:T(128)} %dlen.1, s32[1,2]{1,0:T(1,128)} %order.1, bf16[1,3,1024,256]{3,2,1,0:T(8,128)(2,1)} %w_qkv.1, bf16[1,256,1024]{2,1,0:T(8,128)(2,1)} %w_out.1, ...), custom_call_target="tpu_custom_call" | custom-call | tf_op jit(solution)/shard_map/encode/pallas_call | solution.py:672
  190.3 1.2 split.1

commit v6 on v5

--- a/solution.py
+++ b/solution.py
@@ -9,8 +9,8 @@
 D = 1024
 G = 256
 HALF = 256
-DIRECT = 176
-CHUNKS = ((176, 48), (224, 32))
+DIRECT = 160
+CHUNKS = ((160, 48), (208, 48))
 BF = jnp.bfloat16
 F32 = jnp.float32
 LOG2E = 1.4426950408889634
@@ -409,9 +409,11 @@
     def order_of(t):
         return lax.rem(2 + 3 * t + 3 * (t // 2) + 2 * (t // 3), 4)
 
-    @pl.loop(0, 2 - first)
+    both = 1 - lax.rem((pipe + 1) // 2, 2)
+
+    @pl.loop(0, 2 - both)
     def _(blk):
-        @pl.loop(0, 2 + 2 * first)
+        @pl.loop(0, 2 + 2 * both)
         def _(t):
             @pl.when((first == 1) & (t == 1))
             def _():
@@ -432,8 +434,8 @@
 
             ahead = order_of(t)
             for v in range(2):
-                group = first * ahead + (1 - first) * (2 * t + v)
-                block = first * v + (1 - first) * blk
+                group = first * ahead + (1 - first) * (2 * lax.rem(t, 2) + v)
+                block = first * v + (1 - first) * (blk + both * (t // 2))
                 rows = pl.ds(pl.multiple_of(block * 256, 256), 256)
                 for hd in range(4):
                     nxt = (hd + 1) % 4
@@ -454,8 +456,8 @@
                 total = pltpu.roll(tf[v], 192, 1)
                 scale = jnp.where(total > 2.0**60, 2.0**-64, 1.0).astype(F32)
                 c = (cf[v] * scale) * (1.0 / (total * scale)) * (1.0 / VSCALE)
-                group = first * (ahead + 4 * ((ahead + 3) // 4)) + (1 - first) * (2 * t + v)
-                block = first * v + (1 - first) * blk
+                group = first * (ahead + 4 * ((ahead + 3) // 4)) + (1 - first) * (2 * lax.rem(t, 2) + v)
+                block = first * v + (1 - first) * (blk + both * (t // 2))
                 ctx[group, pl.ds(pl.multiple_of(block * 256, 256), 256), :] = c.astype(BF)
 
         @pl.when(first == 1)
@@ -468,7 +470,7 @@
             for copy in (*share[1], *share[3], *share_on):
                 copy.wait_recv()
 
-        @pl.loop(0, 1 + first)
+        @pl.loop(0, 1 + both)
         def _(b):
             base = (blk + b) * 256
             rows = pl.ds(pl.multiple_of(base, 256), 256)
@@ -476,51 +478,69 @@
                 cs = slice(n * 256, (n + 1) * 256)
                 acc[rows, cs] = sum(dot(ctx[j, rows, :], b_out[j, :, cs]) for j in range(4))
 
+            for u in range(16):
+                if True:
+                    rr = pl.ds(pl.multiple_of(base + u * 16, 16), 16)
+                    mixed[rr, :] = norm_rows(h[0, rr, :].astype(F32) + acc[rr, :], tile[0:1, :]).astype(BF)
+
+        @pl.when(pipe == 3)
+        def _():
+            @pl.loop(0, 4)
+            def _(j):
+                for n in range(4):
+                    cs = slice(n * 256, (n + 1) * 256)
+                    act[:, cs] = gelu(dot(mixed[...], b_up[j, :, cs])).astype(BF)
+                for n in range(4):
+                    cs = slice(n * 256, (n + 1) * 256)
+                    part = dot(act[...], b_down[j, :, cs])
+                    acc[:, cs] = jnp.where(j == 0, part, acc[:, cs] + part)
+
             @pl.loop(0, 2)
             def _(q):
-                for u in range(4):
-                    rr = pl.ds(pl.multiple_of(base + q * 128 + u * 32, 32), 32)
-                    mixed[rr, :] = norm_rows(h[0, rr, :].astype(F32) + acc[rr, :], tile[0:1, :]).astype(BF)
-
-        @pl.loop(0, 4 + 4 * first)
-        def _(i):
-            j = first * (i // 2) + (1 - first) * i
-            r = first * lax.rem(i, 2) + (1 - first) * blk
-
-            @pl.when((first == 1) & (i == 0))
-            def _():
-                step6()
-
-            @pl.when((first == 1) & (i == 2))
-            def _():
-                step7()
-
-            @pl.when((first == 1) & (i == 6))
-            def _():
-                step8()
-
-            rows = pl.ds(pl.multiple_of(r * HALF, HALF), HALF)
-            for n in range(4):
-                cs = slice(n * 256, (n + 1) * 256)
-                act[:, cs] = gelu(dot(mixed[rows, :], b_up[j, :, cs])).astype(BF)
-            for n in range(4):
-                cs = slice(n * 256, (n + 1) * 256)
-                part = dot(act[...], b_down[j, :, cs])
-                acc[rows, cs] = jnp.where(j == 0, part, acc[rows, cs] + part)
-
-            @pl.when(j == 3)
-            def _():
-                @pl.loop(0, 2)
-                def _(q):
-                    for u in range(4):
-                        rr = pl.ds(pl.multiple_of(r * HALF + q * 128 + u * 32, 32), 32)
-                        hout[rr, :] = norm_rows(mixed[rr, :].astype(F32) + acc[rr, :], tile[8:9, :]).astype(BF)
-
-                for rs in range(nblk):
-
-                    @pl.when((pipe < 3) & (r == rs))
-                    def _():
-                        send_on(rs)
+                for u in range(16):
+                    rr = pl.ds(pl.multiple_of(q * 256 + u * 16, 16), 16)
+                    hout[rr, :] = norm_rows(mixed[rr, :].astype(F32) + acc[rr, :], tile[8:9, :]).astype(BF)
+
+        @pl.when(pipe < 3)
+        def _():
+            @pl.loop(0, 4 + 4 * first)
+            def _(i):
+                j = first * (i // 2) + (1 - first) * i
+                r = first * lax.rem(i, 2) + (1 - first) * blk
+
+                @pl.when((first == 1) & (i == 0))
+                def _():
+                    step6()
+
+                @pl.when((first == 1) & (i == 2))
+                def _():
+                    step7()
+
+                @pl.when((first == 1) & (i == 6))
+                def _():
+                    step8()
+
+                rows = pl.ds(pl.multiple_of(r * HALF, HALF), HALF)
+                for n in range(4):
+                    cs = slice(n * 256, (n + 1) * 256)
+                    act[:HALF, cs] = gelu(dot(mixed[rows, :], b_up[j, :, cs])).astype(BF)
+                for n in range(4):
+                    cs = slice(n * 256, (n + 1) * 256)
+                    part = dot(act[:HALF, :], b_down[j, :, cs])
+                    acc[rows, cs] = jnp.where(j == 0, part, acc[rows, cs] + part)
+
+                @pl.when(j == 3)
+                def _():
+                    for u in range(16):
+                        if True:
+                            rr = pl.ds(pl.multiple_of(r * HALF + u * 16, 16), 16)
+                            hout[rr, :] = norm_rows(mixed[rr, :].astype(F32) + acc[rr, :], tile[8:9, :]).astype(BF)
+
+                    for rs in range(nblk):
+
+                        @pl.when((pipe < 3) & (r == rs))
+                        def _():
+                            send_on(rs)
 
     def t1(k):
         return pltpu.make_async_remote_copy(
@@ -693,7 +713,7 @@
             pltpu.VMEM((2 * (HALF - DIRECT), D), BF),
             pltpu.VMEM((S, D), F32),
             pltpu.VMEM((S, D), BF),
-            pltpu.VMEM((HALF, D), BF),
+            pltpu.VMEM((S, D), BF),
             pltpu.VMEM((2, 8, 128), F32),
             pltpu.VMEM((2, 8, 8, 128), F32),
             pltpu.VMEM((5, 8, 128), F32),

time: 192 us -> 188 us (0.979)
  Pallas kernels: 191 us -> 187 us
    pallas_call x1, Pallas kernels: 190 us -> 186 us  [per_device(): pl.pallas_call(kernel, out_shape=jax.ShapeDtypeStruct((8, 128), F32), in_...]
where the time goes in v6:
time: 188 us
  Pallas kernels  187 us (99%)
    pallas_call x1, Pallas kernels, per_device(): pl.pallas_call(kernel, out_shape=jax.ShapeDtypeStruct((8, 128), F32), in_...  186 us

profile of v6, /device:TPU:0, one launch (start us, length us, event | category | flops | bytes accessed | tf_op | source)
XLA Modules:
  0.0 188.0 jit_solution(9263268333609068857)
XLA Ops:
  0.6 186.2 %encode.1.tile = f32[8,128]{1,0:T(8,128)} custom-call(bf16[2,512,1024]{2,1,0:T(8,128)(2,1)} %states_q.1, bf16[2,512,1024]{2,1,0:T(8,128)(2,1)} %states_d.1, s32[2]{0:T(128)} %qlen.1, s32[2]{0:T(128)} %dlen.1, s32[1,2]{1,0:T(1,128)} %order.1, bf16[1,3,1024,256]{3,2,1,0:T(8,128)(2,1)} %w_qkv.1, bf16[1,256,1024]{2,1,0:T(8,128)(2,1)} %w_out.1, ...), custom_call_target="tpu_custom_call" | custom-call | tf_op jit(solution)/shard_map/encode/pallas_call | solution.py:692
  186.8 1.2 split.1
